TPU v7x, 32 devices: a whole 2x2x4 slice. The times are simulated.
32 devices in a mesh: dp: 16 (over z, y, core), tensor: 2 (over x).
Axes of the slice: x: 2, y: 2, z: 4, core: 2. Of those that a mesh axis runs over, the one named last changes fastest.
Arguments:
- layer_input: bfloat16 [32768, 1024], P(('dp', 'tensor')), may hold values from -6 to 6
- gain_attn: bfloat16 [1024], P(('dp', 'tensor')), may hold values from 0.5 to 1.5
- w_query: bfloat16 [1024, 1024], P('dp', 'tensor'), may hold values from -0.1875 to 0.1875
- w_latent: bfloat16 [1024, 512], P('dp', 'tensor'), may hold values from -0.1875 to 0.1875
- w_key: bfloat16 [2, 256, 512], P('tensor', 'dp'), may hold values from -0.375 to 0.375
- w_value: bfloat16 [2, 256, 512], P('tensor', 'dp'), may hold values from -0.375 to 0.375
- w_output: bfloat16 [1024, 1024], P('tensor', 'dp'), may hold values from -2 to 2
- gain_ffn: bfloat16 [1024], P(('dp', 'tensor')), may hold values from 0.5 to 1.5
- w_gate: bfloat16 [1024, 2816], P('dp', 'tensor'), may hold values from -0.1875 to 0.1875
- w_up: bfloat16 [1024, 2816], P('dp', 'tensor'), may hold values from -0.1875 to 0.1875
- w_down: bfloat16 [2816, 1024], P('tensor', 'dp'), may hold values from -0.109375 to 0.109375
- parents: int32 [16, 13], P('dp'), may hold values from 0 to 4, as said below
- counts: int32 [16, 13], P('dp'), may hold values from 1 to 512, as said below
- upstream_grad: bfloat16 [32768, 1024], P(('dp', 'tensor')), may hold values from -6 to 6
Outputs:
- layer_out: bfloat16 [32768, 1024], P(('dp', 'tensor'))
- input_grad: float32 [32768, 1024], P(('dp', 'tensor'))
- gain_attn_grad: float32 [1024], P(('dp', 'tensor'))
- w_query_grad: float32 [1024, 1024], P('dp', 'tensor')
- w_latent_grad: float32 [1024, 512], P('dp', 'tensor')
- w_key_grad: float32 [2, 256, 512], P('tensor', 'dp')
- w_value_grad: float32 [2, 256, 512], P('tensor', 'dp')
- w_output_grad: float32 [1024, 1024], P('tensor', 'dp')
- gain_ffn_grad: float32 [1024], P(('dp', 'tensor'))
- w_gate_grad: float32 [1024, 2816], P('dp', 'tensor')
- w_up_grad: float32 [1024, 2816], P('dp', 'tensor')
- w_down_grad: float32 [2816, 1024], P('tensor', 'dp')
- rms_stats: float32 [3], replicated
Inputs may be any that keep to these rules, and one draw needn't show every extreme that they name: `parents`: segment 0 is the trunk and names itself, the 4 branches (segments 1 to 4) name segment 0, and each of the 8 leaves names one of the branches. `counts`: A segment's count lies between 1 and its length (512 for the trunk, 128 otherwise); the valid tokens of a segment are its first ones.
All inputs are finite; a program needn't handle non-finite values.
Results may differ from a plain program's by a relative error of at most 0.018.
Values may be sent and summed in bfloat16 or wider, within the bound.
A program may use at most 320 MiB of HBM per device.

v0:
```python
import jax
import jax.numpy as jnp
from jax import lax
from jax.sharding import PartitionSpec as P

E = 64
TRUNK = 512
SEG = 128
NSEG = 13


EPSILON = 1e-06


def exact_dot(left, right):
    return jnp.dot(left, right, precision=lax.Precision.HIGHEST, preferred_element_type=jnp.float32)


def row_tables(parents_row, counts_row, tree_len):
    position = jnp.arange(tree_len, dtype=jnp.int32)
    beyond = position - TRUNK
    segment = jnp.where(position < TRUNK, 0, 1 + beyond // SEG)
    offset = jnp.where(position < TRUNK, position, beyond % SEG)
    seg_ids = jnp.arange(NSEG, dtype=jnp.int32)
    seg_hot = segment[:, None] == seg_ids[None, :]
    seg_limit = jnp.sum(jnp.where(seg_hot, counts_row[None, :], 0), axis=1)
    valid_tok = offset < seg_limit
    parent_hot = (parents_row[:, None] == seg_ids[None, :]).astype(jnp.float32)
    ancestor = (
        jnp.eye(NSEG, dtype=jnp.float32) + parent_hot + exact_dot(parent_hot, parent_hot) > 0.5
    )
    key_ok = (
        exact_dot(ancestor.astype(jnp.float32), seg_hot.astype(jnp.float32).T)
        * valid_tok.astype(jnp.float32)[None, :]
    )
    return (segment, offset, valid_tok, key_ok, seg_hot)


def block_mask(tables, first_row, block_len):
    segment, offset, valid_tok, key_ok, seg_hot = tables
    seg_rows = lax.dynamic_slice_in_dim(segment, first_row, block_len)
    off_rows = lax.dynamic_slice_in_dim(offset, first_row, block_len)
    hot_rows = lax.dynamic_slice_in_dim(seg_hot, first_row, block_len).astype(jnp.float32)
    reach = exact_dot(hot_rows, key_ok) > 0.5
    order = (seg_rows[:, None] != segment[None, :]) | (offset[None, :] <= off_rows[:, None])
    return reach & order


def norm_stats(inputs):
    inverse = lax.rsqrt(jnp.mean(inputs * inputs, axis=-1, keepdims=True) + EPSILON)
    return (inputs * inverse, inverse)


def norm_back(normed_grad, gain_vec, normed, inverse):
    scaled = normed_grad * gain_vec
    inner = jnp.mean(scaled * normed, axis=-1, keepdims=True)
    return (inverse * (scaled - normed * inner), jnp.sum(normed_grad * normed, axis=0))


def local(
    layer_input,
    gain_attn,
    w_query,
    w_latent,
    w_key,
    w_value,
    w_output,
    gain_ffn,
    w_gate,
    w_up,
    w_down,
    parents,
    counts,
    upstream_grad,
):
    row_count = layer_input.shape[0]
    model_width = layer_input.shape[1]
    tree_len = row_count * lax.axis_size("tensor")
    first_local = lax.axis_index("tensor") * row_count
    block_len = min(512, tree_len)
    num_blocks = tree_len // block_len
    score_scale = E ** (-0.5)
    gains = (
        lax.all_gather(gain_attn, ("dp", "tensor"), axis=0, tiled=True),
        lax.all_gather(gain_ffn, ("dp", "tensor"), axis=0, tiled=True),
    )
    gain_one = gains[0].astype(jnp.float32)
    gain_two = gains[1].astype(jnp.float32)
    gathered = (
        lax.all_gather(w_query, "dp", axis=0, tiled=True),
        lax.all_gather(w_latent, "dp", axis=0, tiled=True),
        lax.all_gather(w_key, "dp", axis=1, tiled=True),
        lax.all_gather(w_value, "dp", axis=1, tiled=True),
        lax.all_gather(w_output, "dp", axis=1, tiled=True),
        lax.all_gather(w_gate, "dp", axis=0, tiled=True),
        lax.all_gather(w_up, "dp", axis=0, tiled=True),
        lax.all_gather(w_down, "dp", axis=1, tiled=True),
    )
    query_w, latent_w, key_w, value_w, output_w, gate_w, up_w, down_w = gathered
    groups = key_w.shape[0]
    latent_len = key_w.shape[1]
    head_count = query_w.shape[1] // E
    tables = row_tables(parents[0], counts[0], tree_len)
    local_valid = lax.dynamic_slice_in_dim(tables[2].astype(jnp.float32), first_local, row_count)[
        :, None
    ]
    inputs = layer_input.astype(jnp.float32)
    normed_one, inverse_one = norm_stats(inputs)
    attn_in = (normed_one * gain_one).astype(jnp.bfloat16)
    attn_rows_all = lax.all_gather(attn_in, "tensor", axis=0, tiled=True)
    query_flat = jnp.dot(attn_rows_all, query_w, preferred_element_type=jnp.float32).astype(
        jnp.bfloat16
    )
    latent = jnp.dot(attn_rows_all, latent_w, preferred_element_type=jnp.float32).astype(
        jnp.bfloat16
    )
    latent_groups = latent.reshape(tree_len, groups, latent_len)
    key_heads = (
        jnp.einsum("tgl,glf->tgf", latent_groups, key_w, preferred_element_type=jnp.float32)
        .astype(jnp.bfloat16)
        .reshape(tree_len, head_count, E)
    )
    value_heads = (
        jnp.einsum("tgl,glf->tgf", latent_groups, value_w, preferred_element_type=jnp.float32)
        .astype(jnp.bfloat16)
        .reshape(tree_len, head_count, E)
    )
    query_heads = query_flat.reshape(tree_len, head_count, E)

    def forward_block(first_row):
        query_block = lax.dynamic_slice_in_dim(query_heads, first_row, block_len)
        allowed = block_mask(tables, first_row, block_len)
        scores = (
            jnp.einsum("qhe,khe->hqk", query_block, key_heads, preferred_element_type=jnp.float32)
            * score_scale
        )
        scores = jnp.where(allowed[None], scores, -1e30)
        row_max = jnp.max(scores, axis=-1, keepdims=True)
        shifted = jnp.exp(scores - row_max)
        row_total = jnp.sum(shifted, axis=-1, keepdims=True)
        attn_probs = (shifted / row_total).astype(jnp.bfloat16)
        mixed_out = jnp.einsum(
            "hqk,khe->qhe", attn_probs, value_heads, preferred_element_type=jnp.float32
        )
        return (
            mixed_out.reshape(block_len, head_count * E).astype(jnp.bfloat16),
            (row_max + jnp.log(row_total))[:, :, 0],
        )

    starts = jnp.arange(num_blocks, dtype=jnp.int32) * block_len
    mixed_blocks, lse_blocks = lax.map(forward_block, starts)
    heads_out = mixed_blocks.reshape(tree_len, head_count * E)
    branch = lax.psum_scatter(
        jnp.dot(heads_out, output_w, preferred_element_type=jnp.float32).astype(jnp.bfloat16),
        "tensor",
        scatter_dimension=0,
        tiled=True,
    ).astype(jnp.float32)
    residual = inputs + branch
    normed_two, inverse_two = norm_stats(residual)
    ffn_in = (normed_two * gain_two).astype(jnp.bfloat16)
    ffn_rows_all = lax.all_gather(ffn_in, "tensor", axis=0, tiled=True)
    gate_pre = jnp.dot(ffn_rows_all, gate_w, preferred_element_type=jnp.float32)
    up_proj = jnp.dot(ffn_rows_all, up_w, preferred_element_type=jnp.float32)
    gate_sig = jax.nn.sigmoid(gate_pre)
    gate_act = gate_pre * gate_sig
    hidden = (gate_act * up_proj).astype(jnp.bfloat16)
    ffn_out = lax.psum_scatter(
        jnp.dot(hidden, down_w, preferred_element_type=jnp.float32).astype(jnp.bfloat16),
        "tensor",
        scatter_dimension=0,
        tiled=True,
    ).astype(jnp.float32)
    final_out = (residual + ffn_out).astype(jnp.bfloat16)
    stat_terms = jnp.stack(
        [
            jnp.sum(local_valid * branch * branch),
            jnp.sum(local_valid * residual * residual),
            jnp.sum(local_valid * ffn_out * ffn_out),
            jnp.sum(local_valid),
        ]
    )
    query_w, latent_w, key_w, value_w, output_w, gate_w, up_w, down_w = (
        lax.all_gather(w_query, "dp", axis=0, tiled=True),
        lax.all_gather(w_latent, "dp", axis=0, tiled=True),
        lax.all_gather(w_key, "dp", axis=1, tiled=True),
        lax.all_gather(w_value, "dp", axis=1, tiled=True),
        lax.all_gather(w_output, "dp", axis=1, tiled=True),
        lax.all_gather(w_gate, "dp", axis=0, tiled=True),
        lax.all_gather(w_up, "dp", axis=0, tiled=True),
        lax.all_gather(w_down, "dp", axis=1, tiled=True),
    )
    grad_rows = lax.all_gather(upstream_grad, "tensor", axis=0, tiled=True)
    down_grad = jnp.dot(hidden.T, grad_rows, preferred_element_type=jnp.float32)
    hidden_grad = jnp.dot(grad_rows, down_w.T, preferred_element_type=jnp.float32)
    gate_grad = (hidden_grad * up_proj * gate_sig * (1.0 + gate_pre * (1.0 - gate_sig))).astype(
        jnp.bfloat16
    )
    up_grad = (hidden_grad * gate_act).astype(jnp.bfloat16)
    gate_w_grad = jnp.dot(ffn_rows_all.T, gate_grad, preferred_element_type=jnp.float32)
    up_w_grad = jnp.dot(ffn_rows_all.T, up_grad, preferred_element_type=jnp.float32)
    gate_part = jnp.dot(gate_grad, gate_w.T, preferred_element_type=jnp.float32)
    normed_grad_two = lax.psum_scatter(
        (gate_part + jnp.dot(up_grad, up_w.T, preferred_element_type=jnp.float32)).astype(
            jnp.bfloat16
        ),
        "tensor",
        scatter_dimension=0,
        tiled=True,
    ).astype(jnp.float32)
    residual_part, gain_two_grad = norm_back(normed_grad_two, gain_two, normed_two, inverse_two)
    residual_grad = upstream_grad.astype(jnp.float32) + residual_part
    branch_grad = lax.all_gather(residual_grad.astype(jnp.bfloat16), "tensor", axis=0, tiled=True)
    output_w_grad = jnp.dot(heads_out.T, branch_grad, preferred_element_type=jnp.float32)
    heads_grad = (
        jnp.dot(branch_grad, output_w.T, preferred_element_type=jnp.float32)
        .astype(jnp.bfloat16)
        .reshape(tree_len, head_count, E)
    )

    def backward_step(accumulators, step_item):
        key_acc, value_acc = accumulators
        first_row, lse_block = step_item
        query_block = lax.dynamic_slice_in_dim(query_heads, first_row, block_len)
        grad_block = lax.dynamic_slice_in_dim(heads_grad, first_row, block_len)
        allowed = block_mask(tables, first_row, block_len)
        scores = (
            jnp.einsum("qhe,khe->hqk", query_block, key_heads, preferred_element_type=jnp.float32)
            * score_scale
        )
        scores = jnp.where(allowed[None], scores, -1e30)
        attn_probs = jnp.exp(scores - lse_block[:, :, None])
        prob_grad = jnp.einsum(
            "qhe,khe->hqk", grad_block, value_heads, preferred_element_type=jnp.float32
        )
        row_inner = jnp.sum(attn_probs * prob_grad, axis=-1, keepdims=True)
        score_grad = (attn_probs * (prob_grad - row_inner)).astype(jnp.bfloat16)
        query_part = (
            jnp.einsum("hqk,khe->qhe", score_grad, key_heads, preferred_element_type=jnp.float32)
            * score_scale
        )
        key_acc = (
            key_acc
            + jnp.einsum(
                "hqk,qhe->khe", score_grad, query_block, preferred_element_type=jnp.float32
            )
            * score_scale
        )
        value_acc = value_acc + jnp.einsum(
            "hqk,qhe->khe",
            attn_probs.astype(jnp.bfloat16),
            grad_block,
            preferred_element_type=jnp.float32,
        )
        return (
            (key_acc, value_acc),
            query_part.reshape(block_len, head_count * E).astype(jnp.bfloat16),
        )

    initial = jnp.zeros((tree_len, head_count, E), jnp.float32)
    (key_acc, value_acc), query_parts = lax.scan(
        backward_step, (initial, initial), (starts, lse_blocks)
    )
    query_grad = query_parts.reshape(tree_len, head_count * E)
    key_grad = key_acc.astype(jnp.bfloat16).reshape(tree_len, groups, head_count // groups * E)
    value_grad = value_acc.astype(jnp.bfloat16).reshape(tree_len, groups, head_count // groups * E)
    key_w_grad = jnp.einsum(
        "tgl,tgf->glf", latent_groups, key_grad, preferred_element_type=jnp.float32
    )
    value_w_grad = jnp.einsum(
        "tgl,tgf->glf", latent_groups, value_grad, preferred_element_type=jnp.float32
    )
    latent_grad = jnp.einsum("tgf,glf->tgl", key_grad, key_w, preferred_element_type=jnp.float32)
    latent_grad = latent_grad + jnp.einsum(
        "tgf,glf->tgl", value_grad, value_w, preferred_element_type=jnp.float32
    )
    latent_grad = latent_grad.astype(jnp.bfloat16).reshape(tree_len, groups * latent_len)
    query_w_grad = jnp.dot(attn_rows_all.T, query_grad, preferred_element_type=jnp.float32)
    latent_w_grad = jnp.dot(attn_rows_all.T, latent_grad, preferred_element_type=jnp.float32)
    query_part = jnp.dot(query_grad, query_w.T, preferred_element_type=jnp.float32)
    normed_grad_one = lax.psum_scatter(
        (query_part + jnp.dot(latent_grad, latent_w.T, preferred_element_type=jnp.float32)).astype(
            jnp.bfloat16
        ),
        "tensor",
        scatter_dimension=0,
        tiled=True,
    ).astype(jnp.float32)
    input_part, gain_one_grad = norm_back(normed_grad_one, gain_one, normed_one, inverse_one)
    input_grad = residual_grad + input_part
    attn_grads = (
        lax.psum_scatter(query_w_grad, "dp", scatter_dimension=0, tiled=True),
        lax.psum_scatter(latent_w_grad, "dp", scatter_dimension=0, tiled=True),
        lax.psum_scatter(key_w_grad, "dp", scatter_dimension=1, tiled=True),
        lax.psum_scatter(value_w_grad, "dp", scatter_dimension=1, tiled=True),
        lax.psum_scatter(output_w_grad, "dp", scatter_dimension=1, tiled=True),
    )
    ffn_grads = (
        lax.psum_scatter(gate_w_grad, "dp", scatter_dimension=0, tiled=True),
        lax.psum_scatter(up_w_grad, "dp", scatter_dimension=0, tiled=True),
        lax.psum_scatter(down_grad, "dp", scatter_dimension=1, tiled=True),
    )
    small_totals = lax.psum((gain_one_grad, gain_two_grad, stat_terms), ("dp", "tensor"))
    slice_len = gain_attn.shape[0]
    own_start = lax.axis_index(("dp", "tensor")) * slice_len
    gain_attn_grad = lax.dynamic_slice_in_dim(small_totals[0], own_start, slice_len)
    gain_ffn_grad = lax.dynamic_slice_in_dim(small_totals[1], own_start, slice_len)
    stat_totals = small_totals[2]
    rms_stats = jnp.sqrt(stat_totals[:3] / (stat_totals[3] * model_width))
    return (
        final_out,
        input_grad,
        gain_attn_grad,
        attn_grads[0],
        attn_grads[1],
        attn_grads[2],
        attn_grads[3],
        attn_grads[4],
        gain_ffn_grad,
        ffn_grads[0],
        ffn_grads[1],
        ffn_grads[2],
        rms_stats,
    )


def solution(mesh):
    placed = (
        P(("dp", "tensor"), None),
        P(("dp", "tensor")),
        P("dp", "tensor"),
        P("dp", "tensor"),
        P("tensor", "dp", None),
        P("tensor", "dp", None),
        P("tensor", "dp"),
        P(("dp", "tensor")),
        P("dp", "tensor"),
        P("dp", "tensor"),
        P("tensor", "dp"),
        P("dp", None),
        P("dp", None),
        P(("dp", "tensor"), None),
    )
    return jax.shard_map(
        local,
        mesh=mesh,
        in_specs=placed,
        out_specs=(
            P(("dp", "tensor"), None),
            P(("dp", "tensor"), None),
            P(("dp", "tensor")),
            P("dp", "tensor"),
            P("dp", "tensor"),
            P("tensor", "dp", None),
            P("tensor", "dp", None),
            P("tensor", "dp"),
            P(("dp", "tensor")),
            P("dp", "tensor"),
            P("dp", "tensor"),
            P("tensor", "dp"),
            P(),
        ),
        check_vma=False,
    )
```

profile of v0, /device:TPU:0, one launch (start us, length us, event | category | flops | bytes accessed | tf_op | source)
XLA Modules:
  0.0 2004.2 jit_solution(6860521289517446922)
XLA Ops:
  8.9 42.0 %all-reduce.3 = (bf16[1024]{0:T(1024)(128)(2,1)S(1)}, bf16[1024]{0:T(1024)(128)(2,1)}) all-reduce(bf16[1024]{0:T(1024)(128)(2,1)S(1)} %dynamic-update-slice, bf16[1024]{0:T(1024)(128)(2,1)S(1)} %dynamic-update-slice.1), channel_id=1, replica_groups=mesh['dp'=16,'tensor'=2] {'dp','tensor'}, use_global_device_ids=true, to_apply=%add | all-reduce | flops 2048 | bytes 8192
  59.1 22.0 %all_gather.54 = bf16[1,256,512]{2,1,0:T(8,128)(2,1)S(1)} all-gather(bf16[1,16,512]{2,1,0:T(8,128)(2,1)S(1)} %copy-done.37), channel_id=1, replica_groups=mesh['dp'=16,'tensor'=2] {'dp'}, dimensions={1}, use_global_device_ids=true | all-gather | bytes 278528 | tf_op jit(solution)/shard_map/all_gather | solution.py:92
  81.1 18.1 all_gather.55
  99.3 20.2 %all_gather.53 = bf16[1024,256]{1,0:T(8,128)(2,1)S(1)} all-gather(bf16[64,256]{1,0:T(8,128)(2,1)S(1)} %copy-done.35), channel_id=1, replica_groups=mesh['dp'=16,'tensor'=2] {'dp'}, dimensions={0}, use_global_device_ids=true | all-gather | bytes 557056 | tf_op jit(solution)/shard_map/all_gather | solution.py:91
  126.2 28.0 %all-gather.12.cloned.1.call-done = bf16[1024,512]{1,0:T(8,128)(2,1)} async-done(((bf16[64,512]{1,0:T(8,128)(2,1)}), bf16[1024,512]{1,0:T(8,128)(2,1)}) %all-gather.12.cloned.1.call-update) | async-done | bytes 1048592 | tf_op jit(solution)/shard_map/all_gather | solution.py:90
  161.9 216.8 %while.29 = (s32[]{:T(128)}, bf16[4,512,512]{2,1,0:T(8,128)(2,1)}, f32[4,8,512]{2,1,0:T(8,128)S(1)}, s32[4]{0:T(128)S(1)}, pred[2048,13]{0,1:T(8,128)(4,1)S(1)},...) while((s32[]{:T(128)}, bf16[4,512,512]{2,1,0:T(8,128)(2,1)}, ...), condition=%wide.region_5.6_spmd.clone, body=%wide.region_2.5_spmd.clone.sunk | while | flops 2417225728 | bytes 112496840 | solution.py:151
  167.5 16.0 fusion.161
  183.5 15.0 fusion.162
  198.5 15.7 fusion.163
  221.8 15.8 fusion.161
  252.6 15.7 fusion.163
  275.9 15.8 fusion.161
  291.7 15.0 fusion.162
  306.7 15.7 fusion.163
  330.0 15.8 fusion.161
  360.7 15.7 fusion.163
  385.7 52.9 %reduce-scatter.13.cloned.1.call-done = bf16[1024,1024]{1,0:T(8,128)(2,1)} async-done(((bf16[2048,1024]{1,0:T(8,128)(2,1)}), bf16[1024,1024]{1,0:T(8,128)(2,1)}) %reduce-scatter.13.cloned.1.call-update) | async-done | bytes 2097168 | tf_op jit(solution)/shard_map/reduce_scatter | solution.py:153
  446.4 38.3 %all-gather.20.cloned.1.call-done = bf16[1024,1408]{1,0:T(8,128)(2,1)} async-done(((bf16[64,1408]{1,0:T(8,128)(2,1)}), bf16[1024,1408]{1,0:T(8,128)(2,1)}) %all-gather.20.cloned.1.call-update) | async-done | bytes 2883600 | tf_op jit(solution)/shard_map/all_gather | solution.py:96
  484.7 57.4 %all-gather.16.cloned.1.call-done = bf16[2048,1024]{1,0:T(8,128)(2,1)} async-done(((bf16[1024,1024]{1,0:T(8,128)(2,1)}), bf16[2048,1024]{1,0:T(8,128)(2,1)}) %all-gather.16.cloned.1.call-update) | async-done | bytes 4194320 | tf_op jit(solution)/shard_map/all_gather | solution.py:162
  553.8 34.5 %all-gather.18.cloned.1.call-done = bf16[1024,1408]{1,0:T(8,128)(2,1)} async-done(((bf16[64,1408]{1,0:T(8,128)(2,1)}), bf16[1024,1408]{1,0:T(8,128)(2,1)}) %all-gather.18.cloned.1.call-update) | async-done | bytes 2883600 | tf_op jit(solution)/shard_map/all_gather | solution.py:95
  600.1 45.1 %all-gather.24.cloned.1.call-done = bf16[2048,1024]{1,0:T(8,128)(2,1)} async-done(((bf16[1024,1024]{1,0:T(8,128)(2,1)}), bf16[2048,1024]{1,0:T(8,128)(2,1)}) %all-gather.24.cloned.1.call-update) | async-done | bytes 4194320 | tf_op jit(solution)/shard_map/all_gather | solution.py:193
  645.2 46.3 %all-gather.22.cloned.1.call-done = bf16[1408,1024]{0,1:T(8,128)(2,1)} async-done(((bf16[1408,64]{0,1:T(8,128)(2,1)}), bf16[1408,1024]{0,1:T(8,128)(2,1)}) %all-gather.22.cloned.1.call-update) | async-done | bytes 2883600 | tf_op jit(solution)/shard_map/all_gather | solution.py:97
  691.5 21.3 %multiply_convert_fusion.1 = (bf16[2048,1408]{1,0:T(8,128)(2,1)}, bf16[2048,1408]{1,0:T(8,128)(2,1)}, bf16[2048,1408]{1,0:T(8,128)(2,1)}) fusion(f32[2048,1408]{1,0:T(8,128)} %fusion.73, f32[2048,1408]{1,0:T(8,128)} %fusion.74, bf16[2048,1024]{1,0:T(8,128)(2,1)} %all-gather.24.cloned.1.call-done, bf16[1408,1024]{0,1:T(8,128)(2,1)} %all-gather.22.cloned.1.call-done), kind=kOutput, calls=%fused_computation.40 | convolution fusion | flops 5948833792 | bytes 47448064 | tf_op jit(solution)/shard_map/dot_general | solution.py:195
  732.7 51.9 %reduce-scatter.17.cloned.1.call-done = bf16[1024,1024]{1,0:T(8,128)(2,1)} async-done(((bf16[2048,1024]{1,0:T(8,128)(2,1)}), bf16[1024,1024]{1,0:T(8,128)(2,1)}) %reduce-scatter.17.cloned.1.call-update) | async-done | bytes 2097168 | tf_op jit(solution)/shard_map/reduce_scatter | solution.py:203
  795.2 56.8 %all-gather.26.cloned.1.call-done = bf16[2048,1024]{1,0:T(8,128)(2,1)} async-done(((bf16[1024,1024]{1,0:T(8,128)(2,1)}), bf16[2048,1024]{1,0:T(8,128)(2,1)}) %all-gather.26.cloned.1.call-update) | async-done | bytes 4194320 | tf_op jit(solution)/shard_map/all_gather | solution.py:213
  859.4 446.6 %while.30 = (s32[]{:T(128)}, f32[2048,8,64]{0,2,1:T(8,128)}, f32[2048,8,64]{0,2,1:T(8,128)}, bf16[4,512,512]{2,1,0:T(8,128)(2,1)}, s32[4]{0:T(128)S(1)}, /*index...) while((s32[]{:T(128)}, f32[2048,8,64]{0,2,1:T(8,128)}, ...), condition=%wide.region_13.14_spmd.clone.clone, body=%wide.region_11.13_spmd.clone.clone.sunk | while | flops 5618790400 | bytes 348901664 | solution.py:261
  879.5 26.6 %multiply_reduce_fusion.3 = (f32[8,512]{1,0:T(8,128)S(1)}, f32[8,512,2048]{2,1,0:T(8,128)}) fusion(f32[8,512,2048]{2,1,0:T(8,128)} %fusion.175, f32[8,512]{1,0:T(8,128)S(1)} %dynamic-slice_bitcast_fusion.2, bf16[2048,8,64]{0,2,1:T(8,128)(2,1)} %get-tuple-element.590, bf16[2048,8,64]{0,2,1:T(8,128)(2,1)} %get-tuple-element.585, s32[]{:T(128)S(6)} %select_n.160, ...), kind=kOutput, calls=%fused_computation.18.clone.1 | convolution fusion | flops 1115680768 | bytes 70811648 | tf_op jit(solution)/shard_map/while/body/eval_jaxpr/qhe,khe->hqk/dot_general | solution.py:228
  906.1 27.5 %multiply_convert_fusion.6 = bf16[8,512,2048]{2,1,0:T(8,128)(2,1)} fusion(f32[8,512,2048]{2,1,0:T(8,128)} %get-tuple-element.502, f32[8,512,2048]{2,1,0:T(8,128)} %fusion.175, f32[8,512]{1,0:T(8,128)S(1)} %get-tuple-element.503), kind=kLoop, calls=%fused_computation.17.clone.1 | loop fusion | flops 25165824 | bytes 83902464 | tf_op jit(solution)/shard_map/while/body/eval_jaxpr/convert_element_type | solution.py:237
  933.6 15.8 bitcast_add_fusion.5
  989.1 26.6 %multiply_reduce_fusion.3 = (f32[8,512]{1,0:T(8,128)S(1)}, f32[8,512,2048]{2,1,0:T(8,128)}) fusion(f32[8,512,2048]{2,1,0:T(8,128)} %fusion.175, f32[8,512]{1,0:T(8,128)S(1)} %dynamic-slice_bitcast_fusion.2, bf16[2048,8,64]{0,2,1:T(8,128)(2,1)} %get-tuple-element.590, bf16[2048,8,64]{0,2,1:T(8,128)(2,1)} %get-tuple-element.585, s32[]{:T(128)S(6)} %select_n.160, ...), kind=kOutput, calls=%fused_computation.18.clone.1 | convolution fusion | flops 1115680768 | bytes 70811648 | tf_op jit(solution)/shard_map/while/body/eval_jaxpr/qhe,khe->hqk/dot_general | solution.py:228
  1015.7 27.5 %multiply_convert_fusion.6 = bf16[8,512,2048]{2,1,0:T(8,128)(2,1)} fusion(f32[8,512,2048]{2,1,0:T(8,128)} %get-tuple-element.502, f32[8,512,2048]{2,1,0:T(8,128)} %fusion.175, f32[8,512]{1,0:T(8,128)S(1)} %get-tuple-element.503), kind=kLoop, calls=%fused_computation.17.clone.1 | loop fusion | flops 25165824 | bytes 83902464 | tf_op jit(solution)/shard_map/while/body/eval_jaxpr/convert_element_type | solution.py:237
  1043.2 17.1 bitcast_add_fusion.5
  1101.3 26.6 %multiply_reduce_fusion.3 = (f32[8,512]{1,0:T(8,128)S(1)}, f32[8,512,2048]{2,1,0:T(8,128)}) fusion(f32[8,512,2048]{2,1,0:T(8,128)} %fusion.175, f32[8,512]{1,0:T(8,128)S(1)} %dynamic-slice_bitcast_fusion.2, bf16[2048,8,64]{0,2,1:T(8,128)(2,1)} %get-tuple-element.590, bf16[2048,8,64]{0,2,1:T(8,128)(2,1)} %get-tuple-element.585, s32[]{:T(128)S(6)} %select_n.160, ...), kind=kOutput, calls=%fused_computation.18.clone.1 | convolution fusion | flops 1115680768 | bytes 70811648 | tf_op jit(solution)/shard_map/while/body/eval_jaxpr/qhe,khe->hqk/dot_general | solution.py:228
  1127.9 27.5 %multiply_convert_fusion.6 = bf16[8,512,2048]{2,1,0:T(8,128)(2,1)} fusion(f32[8,512,2048]{2,1,0:T(8,128)} %get-tuple-element.502, f32[8,512,2048]{2,1,0:T(8,128)} %fusion.175, f32[8,512]{1,0:T(8,128)S(1)} %get-tuple-element.503), kind=kLoop, calls=%fused_computation.17.clone.1 | loop fusion | flops 25165824 | bytes 83902464 | tf_op jit(solution)/shard_map/while/body/eval_jaxpr/convert_element_type | solution.py:237
  1155.4 17.1 bitcast_add_fusion.5
  1213.4 26.6 %multiply_reduce_fusion.3 = (f32[8,512]{1,0:T(8,128)S(1)}, f32[8,512,2048]{2,1,0:T(8,128)}) fusion(f32[8,512,2048]{2,1,0:T(8,128)} %fusion.175, f32[8,512]{1,0:T(8,128)S(1)} %dynamic-slice_bitcast_fusion.2, bf16[2048,8,64]{0,2,1:T(8,128)(2,1)} %get-tuple-element.590, bf16[2048,8,64]{0,2,1:T(8,128)(2,1)} %get-tuple-element.585, s32[]{:T(128)S(6)} %select_n.160, ...), kind=kOutput, calls=%fused_computation.18.clone.1 | convolution fusion | flops 1115680768 | bytes 70811648 | tf_op jit(solution)/shard_map/while/body/eval_jaxpr/qhe,khe->hqk/dot_general | solution.py:228
  1240.0 27.5 %multiply_convert_fusion.6 = bf16[8,512,2048]{2,1,0:T(8,128)(2,1)} fusion(f32[8,512,2048]{2,1,0:T(8,128)} %get-tuple-element.502, f32[8,512,2048]{2,1,0:T(8,128)} %fusion.175, f32[8,512]{1,0:T(8,128)S(1)} %get-tuple-element.503), kind=kLoop, calls=%fused_computation.17.clone.1 | loop fusion | flops 25165824 | bytes 83902464 | tf_op jit(solution)/shard_map/while/body/eval_jaxpr/convert_element_type | solution.py:237
  1267.5 17.1 bitcast_add_fusion.5
  1394.5 36.7 %reduce-scatter.15.cloned.1.call-done = bf16[1024,1024]{1,0:T(8,128)(2,1)} async-done(((bf16[2048,1024]{1,0:T(8,128)(2,1)}), bf16[1024,1024]{1,0:T(8,128)(2,1)}) %reduce-scatter.15.cloned.1.call-update) | async-done | bytes 2097168 | tf_op jit(solution)/shard_map/reduce_scatter | solution.py:168
  1443.3 41.1 %all-reduce.2 = (f32[1024]{0:T(1024)S(1)}, f32[1024]{0:T(1024)S(1)}, f32[4]{0:T(128)S(1)}) all-reduce(f32[1024]{0:T(1024)S(1)} %get-tuple-element.273, f32[1024]{0:T(1024)S(1)} %copy-done.36, f32[4]{0:T(128)S(1)} %pad_maximum_fusion), channel_id=1, replica_groups=mesh['dp'=16,'tensor'=2] {'dp','tensor'}, use_global_device_ids=true, to_apply=%region_17.18 | all-reduce | flops 2052 | bytes 16416 | tf_op jit(solution)/shard_map/psum | solution.py:303
  1487.3 30.3 %reduce-scatter.35.cloned.1.call-done = f32[1408,64]{0,1:T(8,128)} async-done(((f32[1408,1024]{0,1:T(8,128)}), f32[1408,64]{0,1:T(8,128)}) %reduce-scatter.35.cloned.1.call-update) | async-done | bytes 360464 | tf_op jit(solution)/shard_map/reduce_scatter | solution.py:301
  1517.7 85.0 %reduce-scatter.31.cloned.1.call-done = f32[64,1408]{1,0:T(8,128)} async-done(((f32[1024,1408]{1,0:T(8,128)}), f32[64,1408]{1,0:T(8,128)}) %reduce-scatter.31.cloned.1.call-update) | async-done | bytes 360464 | tf_op jit(solution)/shard_map/reduce_scatter | solution.py:299
  1602.7 85.0 %reduce-scatter.33.cloned.1.call-done = f32[64,1408]{1,0:T(8,128)} async-done(((f32[1024,1408]{1,0:T(8,128)}), f32[64,1408]{1,0:T(8,128)}) %reduce-scatter.33.cloned.1.call-update) | async-done | bytes 360464 | tf_op jit(solution)/shard_map/reduce_scatter | solution.py:300
  1687.6 59.4 %reduce-scatter.25.cloned.1.call-done = f32[1,16,512]{2,1,0:T(8,128)} async-done(((f32[1,256,512]{2,1,0:T(8,128)}), f32[1,16,512]{2,1,0:T(8,128)}) %reduce-scatter.25.cloned.1.call-update) | async-done | bytes 32784 | tf_op jit(solution)/shard_map/reduce_scatter | solution.py:294
  1747.0 59.2 %reduce-scatter.27.cloned.1.call-done = f32[1,16,512]{2,1,0:T(8,128)} async-done(((f32[1,256,512]{2,1,0:T(8,128)}), f32[1,16,512]{2,1,0:T(8,128)}) %reduce-scatter.27.cloned.1.call-update) | async-done | bytes 32784 | tf_op jit(solution)/shard_map/reduce_scatter | solution.py:295
  1806.2 60.9 %reduce-scatter.23.cloned.1.call-done = f32[64,256]{1,0:T(8,128)} async-done(((f32[1024,256]{1,0:T(8,128)}), f32[64,256]{1,0:T(8,128)}) %reduce-scatter.23.cloned.1.call-update) | async-done | bytes 65552 | tf_op jit(solution)/shard_map/reduce_scatter | solution.py:293
  1867.2 64.9 %reduce-scatter.29.cloned.1.call-done = f32[512,64]{0,1:T(8,128)} async-done(((f32[512,1024]{0,1:T(8,128)}), f32[512,64]{0,1:T(8,128)}) %reduce-scatter.29.cloned.1.call-update) | async-done | bytes 131088 | tf_op jit(solution)/shard_map/reduce_scatter | solution.py:296
  1932.1 65.1 %reduce-scatter.21.cloned.1.call-done = f32[64,512]{1,0:T(8,128)} async-done(((f32[1024,512]{1,0:T(8,128)}), f32[64,512]{1,0:T(8,128)}) %reduce-scatter.21.cloned.1.call-update) | async-done | bytes 131088 | tf_op jit(solution)/shard_map/reduce_scatter | solution.py:292
  (275 shorter events, 409.8 us)
Async XLA Ops:
  7.2 112.4 %all-gather.10.cloned.1.call-start = ((), (), s32[]{:S(2)}) async-start(), calls=%async_computation.12 | async-start | bytes 6291456 | tf_op jit(solution)/shard_map/all_gather | solution.py:110
  50.9 7.8 copy-start.44
  50.9 8.1 copy-start.40
  50.9 8.2 copy-start.37
  51.0 30.2 %copy-start.38 = (bf16[1,16,512]{2,1,0:T(8,128)(2,1)S(1)}, bf16[1,16,512]{2,1,0:T(8,128)(2,1)}, u32[]{:S(2)}) copy-start(bf16[1,16,512]{2,1,0:T(8,128)(2,1)} %param.23) | copy-start | bytes 49156
  51.0 48.3 %copy-start.35 = (bf16[64,256]{1,0:T(8,128)(2,1)S(1)}, bf16[64,256]{1,0:T(8,128)(2,1)}, u32[]{:S(2)}) copy-start(bf16[64,256]{1,0:T(8,128)(2,1)} %param.21) | copy-start | bytes 98308
  57.2 97.0 %all-gather.12.cloned.1.call-start = ((), (), s32[]{:S(2)}) async-start(), calls=%async_computation.13 | async-start | bytes 1114112 | tf_op jit(solution)/shard_map/all_gather | solution.py:90
  57.9 320.8 %all-gather.14.cloned.1.call-start = ((), (), s32[]{:S(2)}) async-start(), calls=%async_computation.14 | async-start | bytes 1114112 | tf_op jit(solution)/shard_map/all_gather | solution.py:94
  58.7 379.9 %reduce-scatter.13.cloned.1.call-start = ((), (), s32[]{:S(2)}) async-start(), calls=%async_computation.15 | async-start | bytes 6291456 | tf_op jit(solution)/shard_map/reduce_scatter | solution.py:153
  59.1 60.5 %copy-start.29 = (f32[2048]{0:T(1024)}, f32[2048]{0:T(1024)S(1)}, u32[]{:S(2)}) copy-start(f32[2048]{0:T(1024)S(1)} %compare_convert_fusion) | copy-start | bytes 24580
  81.1 42.8 %copy-start.14 = (bf16[1,256,512]{2,1,0:T(8,128)(2,1)}, bf16[1,256,512]{2,1,0:T(8,128)(2,1)S(1)}, u32[]{:S(2)}) copy-start(bf16[1,256,512]{2,1,0:T(8,128)(2,1)S(1)} %all_gather.54) | copy-start | bytes 786436
  99.3 23.8 %copy-start.16 = (bf16[1,256,512]{2,1,0:T(8,128)(2,1)}, bf16[1,256,512]{2,1,0:T(8,128)(2,1)S(1)}, u32[]{:S(2)}) copy-start(bf16[1,256,512]{2,1,0:T(8,128)(2,1)S(1)} %all_gather.55) | copy-start | bytes 786436
  385.0 99.7 %all-gather.20.cloned.1.call-start = ((), (), s32[]{:S(2)}) async-start(), calls=%async_computation.18 | async-start | bytes 3063808 | tf_op jit(solution)/shard_map/all_gather | solution.py:96
  385.6 156.4 %all-gather.16.cloned.1.call-start = ((), (), s32[]{:S(2)}) async-start(), calls=%async_computation.16 | async-start | bytes 6291456 | tf_op jit(solution)/shard_map/all_gather | solution.py:162
  385.7 405.2 %copy-start.21 = (f32[1024]{0:T(1024)}, f32[1024]{0:T(1024)S(1)}, u32[]{:S(2)}) copy-start(f32[1024]{0:T(1024)S(1)} %convert_element_type.179) | copy-start | bytes 12292
  442.0 348.9 %copy-start.23 = (f32[1024]{0:T(1024)}, f32[1024]{0:T(1024)S(1)}, u32[]{:S(2)}) copy-start(f32[1024]{0:T(1024)S(1)} %add_rsqrt_fusion) | copy-start | bytes 12292
  444.1 144.2 %all-gather.18.cloned.1.call-start = ((), (), s32[]{:S(2)}) async-start(), calls=%async_computation.17 | async-start | bytes 3063808 | tf_op jit(solution)/shard_map/all_gather | solution.py:95
  444.9 200.3 %all-gather.24.cloned.1.call-start = ((), (), s32[]{:S(2)}) async-start(), calls=%async_computation.21 | async-start | bytes 6291456 | tf_op jit(solution)/shard_map/all_gather | solution.py:193
  445.6 245.9 %all-gather.22.cloned.1.call-start = ((), (), s32[]{:S(2)}) async-start(), calls=%async_computation.19 | async-start | bytes 3063808 | tf_op jit(solution)/shard_map/all_gather | solution.py:97
  446.4 338.2 %reduce-scatter.17.cloned.1.call-start = ((), (), s32[]{:S(2)}) async-start(), calls=%async_computation.22 | async-start | bytes 6291456 | tf_op jit(solution)/shard_map/reduce_scatter | solution.py:203
  712.8 9.8 copy-start.41
  712.8 9.8 copy-start.45
  731.4 120.6 %all-gather.26.cloned.1.call-start = ((), (), s32[]{:S(2)}) async-start(), calls=%async_computation.23 | async-start | bytes 6291456 | tf_op jit(solution)/shard_map/all_gather | solution.py:213
  732.7 62.4 %copy-start.31 = (f32[1024]{0:T(1024)}, f32[1024]{0:T(1024)S(1)}, u32[]{:S(2)}) copy-start(f32[1024]{0:T(1024)S(1)} %get-tuple-element.333) | copy-start | bytes 12292
  784.6 6.4 copy-start.7
  790.9 61.1 %copy-start.43 = (bf16[512,1024]{0,1:T(8,128)(2,1)S(1)}, bf16[512,1024]{0,1:T(8,128)(2,1)}, u32[]{:S(2)}) copy-start(bf16[512,1024]{0,1:T(8,128)(2,1)} %all-gather.14.cloned.1.call-done) | copy-start | bytes 3145732
  795.1 596.1 %reduce-scatter.19.cloned.1.call-start = ((), (), s32[]{:S(2)}) async-start(), calls=%async_computation.24 | async-start | bytes 6291456 | tf_op jit(solution)/shard_map/reduce_scatter | solution.py:281
  949.4 11.3 copy-start
  1060.3 11.3 copy-start
  1172.5 11.3 copy-start
  1284.6 11.3 copy-start
  1320.0 111.2 %reduce-scatter.15.cloned.1.call-start = ((), (), s32[]{:S(2)}) async-start(), calls=%async_computation.20 | async-start | bytes 6291456 | tf_op jit(solution)/shard_map/reduce_scatter | solution.py:168
  1331.5 186.2 %reduce-scatter.35.cloned.1.call-start = ((), (), s32[]{:S(2)}) async-start(), calls=%async_computation.32 | async-start | bytes 6127616 | tf_op jit(solution)/shard_map/reduce_scatter | solution.py:301
  1343.4 259.3 %reduce-scatter.31.cloned.1.call-start = ((), (), s32[]{:S(2)}) async-start(), calls=%async_computation.30 | async-start | bytes 6127616 | tf_op jit(solution)/shard_map/reduce_scatter | solution.py:299
  1355.4 332.2 %reduce-scatter.33.cloned.1.call-start = ((), (), s32[]{:S(2)}) async-start(), calls=%async_computation.31 | async-start | bytes 6127616 | tf_op jit(solution)/shard_map/reduce_scatter | solution.py:300
  1367.4 379.7 %reduce-scatter.25.cloned.1.call-start = ((), (), s32[]{:S(2)}) async-start(), calls=%async_computation.27 | async-start | bytes 557056 | tf_op jit(solution)/shard_map/reduce_scatter | solution.py:294
  1370.1 436.1 %reduce-scatter.27.cloned.1.call-start = ((), (), s32[]{:S(2)}) async-start(), calls=%async_computation.28 | async-start | bytes 557056 | tf_op jit(solution)/shard_map/reduce_scatter | solution.py:295
  1373.5 493.7 %reduce-scatter.23.cloned.1.call-start = ((), (), s32[]{:S(2)}) async-start(), calls=%async_computation.26 | async-start | bytes 1114112 | tf_op jit(solution)/shard_map/reduce_scatter | solution.py:293
  1378.3 553.8 %reduce-scatter.29.cloned.1.call-start = ((), (), s32[]{:S(2)}) async-start(), calls=%async_computation.29 | async-start | bytes 2228224 | tf_op jit(solution)/shard_map/reduce_scatter | solution.py:296
  1384.2 7.0 copy-start.4
  1384.2 7.0 copy-start.26
  1384.2 7.0 copy-start.28
  1384.2 612.9 %reduce-scatter.21.cloned.1.call-start = ((), (), s32[]{:S(2)}) async-start(), calls=%async_computation.25 | async-start | bytes 2228224 | tf_op jit(solution)/shard_map/reduce_scatter | solution.py:292
  1391.2 40.1 %copy-start.22 = (f32[1024]{0:T(1024)S(1)}, f32[1024]{0:T(1024)}, u32[]{:S(2)}) copy-start(f32[1024]{0:T(1024)} %copy-done.21) | copy-start | bytes 12292
  1391.2 40.1 %copy-start.24 = (f32[1024]{0:T(1024)S(1)}, f32[1024]{0:T(1024)}, u32[]{:S(2)}) copy-start(f32[1024]{0:T(1024)} %copy-done.23) | copy-start | bytes 12292
  1391.2 40.1 %copy-start.32 = (f32[1024]{0:T(1024)S(1)}, f32[1024]{0:T(1024)}, u32[]{:S(2)}) copy-start(f32[1024]{0:T(1024)} %copy-done.31) | copy-start | bytes 12292
  1391.2 40.1 %copy-start.34 = (f32[1024]{0:T(1024)S(1)}, f32[1024]{0:T(1024)}, u32[]{:S(2)}) copy-start(f32[1024]{0:T(1024)} %copy-done.33) | copy-start | bytes 12292
  1394.5 48.8 %copy-start.36 = (f32[1024]{0:T(1024)S(1)}, f32[1024]{0:T(1024)}, u32[]{:S(2)}) copy-start(f32[1024]{0:T(1024)} %get-tuple-element.271) | copy-start | bytes 12292
  (22 other events, 63.4 us)
Sparse Core Ops, SparseCore 0:
  57.3 56.7 all-gather.9
  116.3 37.8 all-gather.11
  156.3 36.8 all-gather.13
  385.1 53.3 reduce-scatter.12
  440.7 43.9 all-gather.19
  486.6 55.3 all-gather.15
  544.3 43.9 all-gather.17
  589.8 55.3 all-gather.23
  647.5 43.9 all-gather.21
  731.5 52.9 reduce-scatter.16
  795.2 56.7 all-gather.25
  1320.1 54.3 reduce-scatter.18
  1376.8 54.3 reduce-scatter.14
  1435.6 82.0 reduce-scatter.34
  1522.0 80.6 reduce-scatter.30
  1607.0 80.6 reduce-scatter.32
  1691.6 55.3 reduce-scatter.24
  1751.0 55.1 reduce-scatter.26
  1810.4 56.7 reduce-scatter.22
  1871.3 60.6 reduce-scatter.28
  1936.4 60.7 reduce-scatter.20
where the time goes:
time: 2010 us; the launch traced here: 2000 us
  waiting for transfers between devices  962 us (48%)
  matrix products  615 us (31%)
  other arithmetic  211 us (10%)
  blocking collectives  143 us (7%)
  local copies, waits for them, and re-layouts  40.2 us (2%)
    convert_element_type x4, other arithmetic, backward_step(): score_grad = (attn_probs * (prob_grad - row_inner)).astype(jnp.bfloat16)  110 us
    dot_general x4, matrix products, backward_step(): jnp.einsum('qhe,khe->hqk', query_block, key_heads, preferred_element_type...  106 us
    reduce_scatter x1, waiting for transfers between devices, local(): lax.psum_scatter(up_w_grad, 'dp', scatter_dimension=0, tiled=True)  85 us
    reduce_scatter x1, waiting for transfers between devices, local(): lax.psum_scatter(gate_w_grad, 'dp', scatter_dimension=0, tiled=True)  85 us
    dot_general x4, matrix products, backward_step(): jnp.einsum('hqk,qhe->khe', attn_probs.astype(jnp.bfloat16), grad_block, p...  67.2 us
    reduce_scatter x1, waiting for transfers between devices, local(): lax.psum_scatter(query_w_grad, 'dp', scatter_dimension=0, tiled=True)  65.1 us
    reduce_scatter x1, waiting for transfers between devices, local(): lax.psum_scatter(output_w_grad, 'dp', scatter_dimension=1, tiled=True)  64.9 us
    dot_general x4, matrix products, forward_block(): jnp.einsum('qhe,khe->hqk', query_block, key_heads, preferred_element_type...  63.4 us
  transfers between devices with their start and end apart: 21, of which 18 were waited for; matrix products, arithmetic and copies ran while one was open for 17% of the time, Pallas kernels for 0%

commit v1 on v0

v1 whole, which is shorter than its diff:
```python
import jax
import jax.numpy as jnp
from jax import lax
from jax.experimental import pallas as pl
from jax.experimental.pallas import tpu as pltpu
from jax.sharding import PartitionSpec as P

E = 64
TRUNK = 512
SEG = 128
NSEG = 13
NBRANCH = 4
PAIR = 2 * E
CHUNK = 256
NEG = -1e30
EPSILON = 1e-06

GATHER_AXES = ("tensor", "dp")

NN = (((1,), (0,)), ((), ()))
NT = (((1,), (1,)), ((), ()))
TN = (((0,), (0,)), ((), ()))


def mm(left, right, dims=NN):
    return lax.dot_general(left, right, dims, preferred_element_type=jnp.float32)


def block_scalars(meta_ref, block):
    leaf_side = meta_ref[0] == 1
    segment = jnp.where(leaf_side, block + (1 + NBRANCH), block - (TRUNK // SEG - 1))
    present = segment >= 1
    index = jnp.maximum(segment, 0)
    parent = meta_ref[1 + NSEG + index]
    own_count = jnp.where(present, meta_ref[1 + index], 0)
    parent_count = jnp.where(present & (parent >= 1), meta_ref[1 + parent], 0)
    parent_row = TRUNK + SEG * jnp.maximum(parent - 1, 0)
    return own_count, parent_count, pl.multiple_of(parent_row, SEG)


def trunk_limits(meta_ref, step):
    causal = (meta_ref[0] == 0) & (step < TRUNK // CHUNK)
    return meta_ref[1], jnp.where(causal, step * CHUNK, TRUNK)


def head_masks(dtype, value):
    lane = lax.broadcasted_iota(jnp.int32, (1, PAIR), 1)
    first = jnp.where(lane < E, value, 0.0).astype(dtype)
    second = jnp.where(lane < E, 0.0, value).astype(dtype)
    return first, second


def forward_kernel(meta_ref, q_ref, kv_ref, o_ref, lse_ref):
    step = pl.program_id(1)
    local_rows = kv_ref.shape[0] // 2
    query = q_ref[...]
    scale = head_masks(query.dtype, E ** (-0.5))
    trunk_count, shift = trunk_limits(meta_ref, step)
    key_pos = lax.broadcasted_iota(jnp.int32, (CHUNK, TRUNK), 1)
    row_pos = lax.broadcasted_iota(jnp.int32, (CHUNK, TRUNK), 0)
    trunk_ok = (key_pos <= row_pos + shift) & (key_pos < trunk_count)
    seg_key = lax.broadcasted_iota(jnp.int32, (SEG, SEG), 1)
    seg_row = lax.broadcasted_iota(jnp.int32, (SEG, SEG), 0)
    starts, par_ok, own_ok = [], [], []
    for j in range(CHUNK // SEG):
        block = step * (CHUNK // SEG) + j
        own_count, parent_count, parent_row = block_scalars(meta_ref, block)
        starts.append((parent_row, pl.multiple_of(local_rows + block * SEG, SEG)))
        par_ok.append(seg_key < parent_count)
        own_ok.append((seg_key <= seg_row) & (seg_key < own_count))
    outs, lses = [], []
    for h in range(2):
        qh = query * scale[h]
        trunk = jnp.where(trunk_ok, mm(qh, kv_ref[0:TRUNK, 0:PAIR], NT), NEG)
        par, own = [], []
        for j, (first, second) in enumerate(starts):
            qj = qh[j * SEG : (j + 1) * SEG]
            par.append(jnp.where(par_ok[j], mm(qj, kv_ref[pl.ds(first, SEG), 0:PAIR], NT), NEG))
            own.append(jnp.where(own_ok[j], mm(qj, kv_ref[pl.ds(second, SEG), 0:PAIR], NT), NEG))
        par_all = jnp.concatenate(par, axis=0)
        own_all = jnp.concatenate(own, axis=0)
        top = jnp.maximum(par_all, own_all)
        for i in range(TRUNK // SEG):
            top = jnp.maximum(top, trunk[:, i * SEG : (i + 1) * SEG])
        top = jnp.max(top, axis=1, keepdims=True)
        trunk = jnp.exp(trunk - top)
        par_all = jnp.exp(par_all - top)
        own_all = jnp.exp(own_all - top)
        total = par_all + own_all
        for i in range(TRUNK // SEG):
            total = total + trunk[:, i * SEG : (i + 1) * SEG]
        total = jnp.sum(total, axis=1, keepdims=True)
        out = mm(trunk.astype(jnp.bfloat16), kv_ref[0:TRUNK, PAIR : 2 * PAIR])
        tails = []
        for j, (first, second) in enumerate(starts):
            part = slice(j * SEG, (j + 1) * SEG)
            tails.append(
                mm(par_all[part].astype(jnp.bfloat16), kv_ref[pl.ds(first, SEG), PAIR : 2 * PAIR])
                + mm(own_all[part].astype(jnp.bfloat16), kv_ref[pl.ds(second, SEG), PAIR : 2 * PAIR])
            )
        out = out + jnp.concatenate(tails, axis=0)
        outs.append(out * (1.0 / total))
        lses.append(jnp.broadcast_to(top + jnp.log(total), (CHUNK, PAIR)))
    lane = lax.broadcasted_iota(jnp.int32, (CHUNK, PAIR), 1)
    o_ref[...] = jnp.where(lane < E, outs[0], outs[1]).astype(o_ref.dtype)
    turned = jnp.transpose(jnp.where(lane < E, lses[0], lses[1]))
    lse_ref[0, 0:1, :] = turned[0:1, :]
    lse_ref[0, 1:2, :] = turned[E : E + 1, :]


def attend_forward(meta, query, kv):
    rows, width = query.shape
    pairs = width // PAIR
    return pl.pallas_call(
        forward_kernel,
        grid_spec=pltpu.PrefetchScalarGridSpec(
            num_scalar_prefetch=1,
            grid=(pairs, rows // CHUNK),
            in_specs=[
                pl.BlockSpec((CHUNK, PAIR), lambda p, c, meta: (c, p)),
                pl.BlockSpec((2 * rows, 2 * PAIR), lambda p, c, meta: (0, p)),
            ],
            out_specs=[
                pl.BlockSpec((CHUNK, PAIR), lambda p, c, meta: (c, p)),
                pl.BlockSpec((1, 2, CHUNK), lambda p, c, meta: (p, 0, c)),
            ],
        ),
        out_shape=[
            jax.ShapeDtypeStruct((rows, width), jnp.bfloat16),
            jax.ShapeDtypeStruct((pairs, 2, rows), jnp.float32),
        ],
        name="attend_forward",
    )(meta, query, kv)


def backward_kernel(meta_ref, q_ref, kv_ref, o_ref, do_ref, lse_ref, dq_ref, dkv_ref, acc_ref):
    step = pl.program_id(1)
    local_rows = kv_ref.shape[0] // 2

    @pl.when(step == 0)
    def _():
        acc_ref[...] = jnp.zeros_like(acc_ref)

    query = q_ref[...]
    grad = do_ref[...]
    scale = head_masks(query.dtype, E ** (-0.5))
    keep = head_masks(query.dtype, 1.0)
    product = jnp.transpose(grad.astype(jnp.float32) * o_ref[...].astype(jnp.float32))
    trunk_count, shift = trunk_limits(meta_ref, step)
    key_pos = lax.broadcasted_iota(jnp.int32, (TRUNK, CHUNK), 0)
    row_pos = lax.broadcasted_iota(jnp.int32, (TRUNK, CHUNK), 1)
    trunk_ok = (key_pos <= row_pos + shift) & (key_pos < trunk_count)
    seg_key = lax.broadcasted_iota(jnp.int32, (SEG, SEG), 0)
    seg_row = lax.broadcasted_iota(jnp.int32, (SEG, SEG), 1)
    blocks = []
    for j in range(CHUNK // SEG):
        block = step * (CHUNK // SEG) + j
        own_count, parent_count, parent_row = block_scalars(meta_ref, block)
        own_row = pl.multiple_of(local_rows + block * SEG, SEG)
        blocks.append(
            (
                (parent_row, seg_key < parent_count),
                (own_row, (seg_key <= seg_row) & (seg_key < own_count)),
            )
        )
    query_grads = []
    trunk_parts = []
    block_parts = [[[], []] for _ in blocks]
    for h in range(2):
        qh = query * scale[h]
        gh = grad * keep[h]
        lse = lse_ref[0, h : h + 1, :]
        inner = jnp.sum(product[h * E : (h + 1) * E], axis=0, keepdims=True)

        def part(rows, allowed, qs, gs, lse_row, inner_row):
            keys = kv_ref[rows, 0:PAIR]
            values = kv_ref[rows, PAIR : 2 * PAIR]
            scores = jnp.where(allowed, mm(keys, qs, NT), NEG)
            probs = jnp.exp(scores - lse_row)
            score_grad = (probs * (mm(values, gs, NT) - inner_row)).astype(jnp.bfloat16)
            return (
                mm(score_grad, keys, TN),
                mm(score_grad, qs),
                mm(probs.astype(jnp.bfloat16), gs),
            )

        query_grad, key_part, value_part = part(slice(0, TRUNK), trunk_ok, qh, gh, lse, inner)
        trunk_parts.append((key_part, value_part))
        tails = []
        for j, sources in enumerate(blocks):
            cut = slice(j * SEG, (j + 1) * SEG)
            tail = 0.0
            for k, (first, allowed) in enumerate(sources):
                moved, key_part, value_part = part(
                    pl.ds(first, SEG), allowed, qh[cut], gh[cut], lse[:, cut], inner[:, cut]
                )
                tail = tail + moved
                block_parts[j][k].append((key_part, value_part))
            tails.append(tail)
        query_grads.append(query_grad + jnp.concatenate(tails, axis=0))
    lane = lax.broadcasted_iota(jnp.int32, (CHUNK, PAIR), 1)
    dq_ref[...] = (jnp.where(lane < E, query_grads[0], query_grads[1]) * E ** (-0.5)).astype(
        dq_ref.dtype
    )
    for side in range(2):
        cols = slice(side * PAIR, (side + 1) * PAIR)
        acc_ref[0:TRUNK, cols] += trunk_parts[0][side] + trunk_parts[1][side]
        for j, sources in enumerate(blocks):
            for k, (first, _) in enumerate(sources):
                both = block_parts[j][k][0][side] + block_parts[j][k][1][side]
                if k == 0:
                    acc_ref[pl.ds(first, SEG), cols] += both
                else:
                    dkv_ref[pl.ds(first, SEG), cols] = both.astype(dkv_ref.dtype)

    @pl.when(step == pl.num_programs(1) - 1)
    def _():
        dkv_ref[0:local_rows, :] = acc_ref[...].astype(dkv_ref.dtype)


def attend_backward(meta, query, kv, out, grad, lse):
    rows, width = query.shape
    pairs = width // PAIR
    row_spec = pl.BlockSpec((CHUNK, PAIR), lambda p, c, meta: (c, p))
    kv_spec = pl.BlockSpec((2 * rows, 2 * PAIR), lambda p, c, meta: (0, p))
    return pl.pallas_call(
        backward_kernel,
        grid_spec=pltpu.PrefetchScalarGridSpec(
            num_scalar_prefetch=1,
            grid=(pairs, rows // CHUNK),
            in_specs=[
                row_spec,
                kv_spec,
                row_spec,
                row_spec,
                pl.BlockSpec((1, 2, CHUNK), lambda p, c, meta: (p, 0, c)),
            ],
            out_specs=[row_spec, kv_spec],
            scratch_shapes=[pltpu.VMEM((rows, 2 * PAIR), jnp.float32)],
        ),
        out_shape=[
            jax.ShapeDtypeStruct((rows, width), jnp.bfloat16),
            jax.ShapeDtypeStruct((2 * rows, 2 * width), jnp.bfloat16),
        ],
        name="attend_backward",
    )(meta, query, kv, out, grad, lse)


def norm_stats(inputs):
    inverse = lax.rsqrt(jnp.mean(inputs * inputs, axis=-1, keepdims=True) + EPSILON)
    return (inputs * inverse, inverse)


def norm_back(normed_grad, gain_vec, normed, inverse):
    scaled = normed_grad * gain_vec
    inner = jnp.mean(scaled * normed, axis=-1, keepdims=True)
    return (inverse * (scaled - normed * inner), jnp.sum(normed_grad * normed, axis=0))


def interleave(keys, values):
    rows, width = keys.shape
    shape = (rows, width // PAIR, 1, PAIR)
    both = jnp.concatenate([keys.reshape(shape), values.reshape(shape)], axis=2)
    return both.reshape(rows, 2 * width)


def scatter(parts):
    return lax.psum_scatter(
        jnp.concatenate(parts, axis=0), GATHER_AXES, scatter_dimension=0, tiled=True
    )


def local(
    layer_input,
    gain_attn,
    w_query,
    w_latent,
    w_key,
    w_value,
    w_output,
    gain_ffn,
    w_gate,
    w_up,
    w_down,
    parents,
    counts,
    upstream_grad,
):
    bf16 = jnp.bfloat16
    row_count, model_width = layer_input.shape
    sides = lax.axis_size("tensor")
    dp_size = lax.axis_size("dp")
    side = lax.axis_index("tensor")
    shard_rows, query_len = w_query.shape
    latent_len = w_latent.shape[1]
    hidden_len = w_gate.shape[1]
    kv_rows, kv_len = w_key.shape[1:]
    gain_len = gain_attn.shape[0]
    kv_cols = kv_rows * 2 * kv_len // shard_rows
    gain_cols = 2 * E

    meta = jnp.concatenate([side[None].astype(jnp.int32), counts[0], parents[0]])

    sent = lax.ppermute(layer_input, "tensor", [(0, 1)])

    gain_row = jnp.concatenate([gain_attn, gain_ffn])[None, :]
    gain_block = jnp.pad(gain_row, ((0, shard_rows - 1), (0, gain_cols - 2 * gain_len)))
    attn_pack = jnp.concatenate(
        [
            w_query,
            w_latent,
            w_output.T,
            interleave(w_key[0], w_value[0]).reshape(shard_rows, kv_cols),
            gain_block,
        ],
        axis=1,
    )
    attn_all = lax.all_gather(attn_pack, GATHER_AXES, axis=0, tiled=True)
    gate_up_all = lax.all_gather(
        jnp.concatenate([w_gate, w_up], axis=1), GATHER_AXES, axis=0, tiled=True
    )
    down_all = lax.all_gather(w_down.T, GATHER_AXES, axis=0, tiled=True)

    def part_of(gathered, t, first, size):
        return lax.slice(
            gathered, (t * model_width, first), ((t + 1) * model_width, first + size)
        )

    first_latent = query_len
    first_out = first_latent + latent_len
    first_kv = first_out + query_len
    first_gain = first_kv + kv_cols
    query_w = [part_of(attn_all, t, 0, query_len) for t in range(sides)]
    latent_w = [part_of(attn_all, t, first_latent, latent_len) for t in range(sides)]
    out_w = [part_of(attn_all, t, first_out, query_len) for t in range(sides)]
    kv_w = [
        part_of(attn_all, t, first_kv, kv_cols).reshape(dp_size * kv_rows, 2 * kv_len)
        for t in range(sides)
    ]
    gains = attn_all[:, first_gain : first_gain + 2 * gain_len]
    gains = gains.reshape(sides, dp_size, shard_rows, 2, gain_len)[:, :, 0]
    gains = gains.transpose(2, 1, 0, 3).reshape(2, model_width).astype(jnp.float32)
    gain_one, gain_two = gains[0], gains[1]
    gate_w = [part_of(gate_up_all, t, 0, hidden_len) for t in range(sides)]
    up_w = [part_of(gate_up_all, t, hidden_len, hidden_len) for t in range(sides)]
    down_w = [part_of(down_all, t, 0, hidden_len) for t in range(sides)]

    context_input = jnp.where(side == 0, layer_input, sent)
    inputs = layer_input.astype(jnp.float32)
    normed_one, inverse_one = norm_stats(inputs)
    attn_in = (normed_one * gain_one).astype(bf16)
    context_in = (norm_stats(context_input.astype(jnp.float32))[0] * gain_one).astype(bf16)
    both_in = jnp.concatenate([context_in, attn_in], axis=0)
    queries, latents, kvs, heads, lses = [], [], [], [], []
    for t in range(sides):
        latents.append(mm(both_in, latent_w[t]).astype(bf16))
        queries.append(mm(attn_in, query_w[t]).astype(bf16))
        kvs.append(mm(latents[t], kv_w[t]).astype(bf16))
        out, lse = attend_forward(meta, queries[t], kvs[t])
        heads.append(out)
        lses.append(lse)
    branch = sum(mm(heads[t], out_w[t], NT) for t in range(sides))
    residual = inputs + branch
    normed_two, inverse_two = norm_stats(residual)
    ffn_in = (normed_two * gain_two).astype(bf16)

    gates = [mm(ffn_in, gate_w[t]) for t in range(sides)]
    ups = [mm(ffn_in, up_w[t]) for t in range(sides)]
    sigs = [jax.nn.sigmoid(gate) for gate in gates]
    hiddens = [(gates[t] * sigs[t] * ups[t]).astype(bf16) for t in range(sides)]
    ffn_out = sum(mm(hiddens[t], down_w[t], NT) for t in range(sides))
    final_out = (residual + ffn_out).astype(bf16)
    down_grads = [mm(upstream_grad, hiddens[t], TN).astype(bf16) for t in range(sides)]
    down_sum = scatter(down_grads)

    position = side * row_count + lax.broadcasted_iota(jnp.int32, (row_count, NSEG), 0)
    seg_ids = lax.broadcasted_iota(jnp.int32, (row_count, NSEG), 1)
    beyond = position - TRUNK
    segment = jnp.where(beyond < 0, 0, 1 + beyond // SEG)
    offset = jnp.where(beyond < 0, position, beyond % SEG)
    valid = jnp.any((segment == seg_ids) & (offset < counts[0][None, :]), axis=1, keepdims=True)
    valid = valid.astype(jnp.float32)
    stat_terms = jnp.stack(
        [
            jnp.sum(valid * branch * branch),
            jnp.sum(valid * residual * residual),
            jnp.sum(valid * ffn_out * ffn_out),
            jnp.sum(valid),
        ]
    )
    stat_rows = jnp.broadcast_to(jnp.pad(stat_terms, (0, 2 * E - 4))[None, :], (8, 2 * E))
    stat_all = lax.all_gather(stat_rows, GATHER_AXES, axis=0, tiled=True)
    stat_totals = jnp.sum(stat_all.reshape(sides * dp_size, 8, 2 * E)[:, 0, :4], axis=0)
    rms_stats = jnp.sqrt(stat_totals[:3] / (stat_totals[3] * model_width))

    ffn_grads = []
    normed_grad_two = 0.0
    for t in range(sides):
        hidden_grad = mm(upstream_grad, down_w[t])
        gate_act = gates[t] * sigs[t]
        gate_grad = (
            hidden_grad * ups[t] * sigs[t] * (1.0 + gates[t] * (1.0 - sigs[t]))
        ).astype(bf16)
        up_grad = (hidden_grad * gate_act).astype(bf16)
        normed_grad_two = (
            normed_grad_two + mm(gate_grad, gate_w[t], NT) + mm(up_grad, up_w[t], NT)
        )
        ffn_grads.append((mm(ffn_in, gate_grad, TN).astype(bf16), mm(ffn_in, up_grad, TN).astype(bf16)))
    gate_sum = scatter([pair[0] for pair in ffn_grads])
    up_sum = scatter([pair[1] for pair in ffn_grads])
    residual_part, gain_two_grad = norm_back(normed_grad_two, gain_two, normed_two, inverse_two)
    residual_grad = upstream_grad.astype(jnp.float32) + residual_part
    branch_grad = residual_grad.astype(bf16)

    attn_grads = []
    normed_grad_one = 0.0
    for t in range(sides):
        out_grad = mm(branch_grad, heads[t], TN).astype(bf16)
        heads_grad = mm(branch_grad, out_w[t]).astype(bf16)
        query_grad, kv_grad = attend_backward(
            meta, queries[t], kvs[t], heads[t], heads_grad, lses[t]
        )
        latent_part = mm(kv_grad, kv_w[t], NT)
        context_part = latent_part[:row_count]
        returned = lax.ppermute(context_part.astype(bf16), "tensor", [(1, 0)])
        kv_w_grad = mm(latents[t], kv_grad, TN).astype(bf16)
        query_w_grad = mm(attn_in, query_grad, TN).astype(bf16)
        latent_grad = (
            latent_part[row_count:]
            + jnp.where(side == 0, context_part, 0.0)
            + returned.astype(jnp.float32)
        ).astype(bf16)
        latent_w_grad = mm(attn_in, latent_grad, TN).astype(bf16)
        normed_grad_one = (
            normed_grad_one + mm(query_grad, query_w[t], NT) + mm(latent_grad, latent_w[t], NT)
        )
        attn_grads.append(
            [query_w_grad, latent_w_grad, out_grad, kv_w_grad.reshape(model_width, kv_cols)]
        )
    input_part, gain_one_grad = norm_back(normed_grad_one, gain_one, normed_one, inverse_one)
    input_grad = residual_grad + input_part

    gain_grads = jnp.stack([gain_one_grad, gain_two_grad]).reshape(2, dp_size, sides, gain_len)
    gain_grads = gain_grads.transpose(2, 1, 0, 3).reshape(sides, dp_size, 1, 2 * gain_len)
    gain_grads = jnp.pad(
        gain_grads.astype(bf16),
        ((0, 0), (0, 0), (0, shard_rows - 1), (0, gain_cols - 2 * gain_len)),
    ).reshape(sides, model_width, gain_cols)
    attn_sum = scatter(
        [jnp.concatenate(attn_grads[t] + [gain_grads[t]], axis=1) for t in range(sides)]
    ).astype(jnp.float32)
    kv_sum = attn_sum[:, first_kv:first_gain].reshape(kv_rows, kv_len // PAIR, 2, PAIR)
    return (
        final_out,
        input_grad,
        attn_sum[0, first_gain : first_gain + gain_len],
        attn_sum[:, :query_len],
        attn_sum[:, first_latent:first_out],
        kv_sum[:, :, 0].reshape(1, kv_rows, kv_len),
        kv_sum[:, :, 1].reshape(1, kv_rows, kv_len),
        attn_sum[:, first_out:first_kv].T,
        attn_sum[0, first_gain + gain_len : first_gain + 2 * gain_len],
        gate_sum.astype(jnp.float32),
        up_sum.astype(jnp.float32),
        down_sum.astype(jnp.float32).T,
        rms_stats,
    )


def solution(mesh):
    placed = (
        P(("dp", "tensor"), None),
        P(("dp", "tensor")),
        P("dp", "tensor"),
        P("dp", "tensor"),
        P("tensor", "dp", None),
        P("tensor", "dp", None),
        P("tensor", "dp"),
        P(("dp", "tensor")),
        P("dp", "tensor"),
        P("dp", "tensor"),
        P("tensor", "dp"),
        P("dp", None),
        P("dp", None),
        P(("dp", "tensor"), None),
    )
    return jax.shard_map(
        local,
        mesh=mesh,
        in_specs=placed,
        out_specs=(
            P(("dp", "tensor"), None),
            P(("dp", "tensor"), None),
            P(("dp", "tensor")),
            P("dp", "tensor"),
            P("dp", "tensor"),
            P("tensor", "dp", None),
            P("tensor", "dp", None),
            P("tensor", "dp"),
            P(("dp", "tensor")),
            P("dp", "tensor"),
            P("dp", "tensor"),
            P("tensor", "dp"),
            P(),
        ),
        check_vma=False,
    )
```

time: 2010 us -> 901 us (0.45)
  waiting for transfers between devices: 962 us -> 396 us
  matrix products: 615 us -> 196 us
  other arithmetic: 211 us -> 41.1 us
  Pallas kernels: 0 us -> 131 us
  blocking collectives: 143 us -> 43.1 us
  local copies, waits for them, and re-layouts: 40.2 us -> 62.2 us
    reduce_scatter x12 -> x3, waiting for transfers between devices: 651 us -> 114 us  [scatter(): lax.psum_scatter(jnp.concatenate(parts, axis=0), GATHER_AXES, scatter_dim...]
    dot_general x62 -> x42, matrix products: 615 us -> 196 us  [mm(): lax.dot_general(left, right, dims, preferred_element_type=jnp.float32)]
    all_gather x9 -> x3, waiting for transfers between devices: 306 us -> 78.8 us  [the longest x1 69.2 us: local(): attn_all = lax.all_gather(attn_pack, GATHER_AXES, axis=0, tiled=True)]
    unnamed x21 -> x8, waiting for transfers between devices: 4.23 us -> 145 us
    pallas_call x0 -> x4, Pallas kernels: none -> 131 us  [the longest x2 85.8 us: attend_backward(): pl.pallas_call(backward_kernel, grid_spec=pltpu.PrefetchScalarGridSpec(nu...]
    convert_element_type x12 -> x11, other arithmetic: 122 us -> 8.81 us  [the longest x2 2.74 us: local(): latent_grad = (latent_part[row_count:] + jnp.where(side == 0, context_par...]
    reduce_sum x8 -> x2, other arithmetic: 70.3 us -> 0.65 us  [the longest x1 0.6 us: local(): jnp.sum(valid)]
    ppermute x0 -> x3, waiting for transfers between devices: none -> 59.4 us  [the longest x1 59.4 us: local(): sent = lax.ppermute(layer_input, 'tensor', [(0, 1)])]
  transfers between devices with their start and end apart: 21 -> 10, of which waited for: 18 -> 5; matrix products, arithmetic and copies ran while one was open for 17% -> 27% of each run, Pallas kernels for 0% -> 15%
where the time goes in v1:
time: 901 us; the launch traced here: 895 us
  waiting for transfers between devices  396 us (44%)
  matrix products  196 us (22%)
  Pallas kernels  131 us (15%)
  local copies, waits for them, and re-layouts  62.2 us (7%)
  blocking collectives  43.1 us (5%)
  other arithmetic  41.1 us (5%)
  between operations  16.1 us (2%)
  starting transfers between devices  9.25 us (1%)
    dot_general x42, matrix products, mm(): lax.dot_general(left, right, dims, preferred_element_type=jnp.float32)  196 us
    unnamed x8, waiting for transfers between devices  145 us
    reduce_scatter x3, waiting for transfers between devices, scatter(): lax.psum_scatter(jnp.concatenate(parts, axis=0), GATHER_AXES, scatter_dim...  114 us
    pallas_call x2, Pallas kernels, attend_backward(): pl.pallas_call(backward_kernel, grid_spec=pltpu.PrefetchScalarGridSpec(nu...  85.8 us
    all_gather x1, waiting for transfers between devices, local(): attn_all = lax.all_gather(attn_pack, GATHER_AXES, axis=0, tiled=True)  69.2 us
    ppermute x1, waiting for transfers between devices, local(): sent = lax.ppermute(layer_input, 'tensor', [(0, 1)])  59.4 us
    pallas_call x2, Pallas kernels, attend_forward(): pl.pallas_call(forward_kernel, grid_spec=pltpu.PrefetchScalarGridSpec(num...  45 us
    all_gather x1, blocking collectives, local(): stat_all = lax.all_gather(stat_rows, GATHER_AXES, axis=0, tiled=True)  43.1 us
  transfers between devices with their start and end apart: 10, of which 5 were waited for; matrix products, arithmetic and copies ran while one was open for 27% of the time, Pallas kernels for 15%

profile of v1, /device:TPU:0, one launch (start us, length us, event | category | flops | bytes accessed | tf_op | source)
XLA Modules:
  0.0 895.5 jit_solution(10875787856387299938)
XLA Ops:
  18.2 6.2 collective-permute-start
  25.0 59.4 %collective-permute-done = bf16[1024,1024]{0,1:T(8,128)(2,1)} collective-permute-done((bf16[1024,1024]{0,1:T(8,128)(2,1)S(1)}, bf16[1024,1024]{0,1:T(8,128)(2,1)}, u32[]{:S(2)}, u32[]{:S(2)}) %collective-permute-start) | collective-permute-done | bytes 2097184 | tf_op jit(solution)/shard_map/ppermute | solution.py:304
  85.6 8.6 fusion.37
  94.1 5.4 fusion.25
  99.6 69.2 %all-gather.4.cloned.1.call-done = bf16[2048,1664]{1,0:T(8,128)(2,1)} async-done(((bf16[64,1664]{1,0:T(8,128)(2,1)}), bf16[2048,1664]{1,0:T(8,128)(2,1)}) %all-gather.4.cloned.1.call-update) | async-done | bytes 6815760 | tf_op jit(solution)/shard_map/all_gather | solution.py:318
  179.5 3.3 convolution_convert_fusion.kv_ref
  182.8 3.5 convolution_convert_fusion.14.q_ref
  186.3 22.8 %attend_forward.3 = (bf16[1024,512]{1,0:T(8,128)(2,1)}, f32[4,2,1024]{2,1,0:T(2,128)}) custom-call(s32[27]{0:T(128)} %pad_add_fusion.meta_ref, bf16[1024,512]{1,0:T(8,128)(2,1)} %convolution_convert_fusion.14.q_ref, bf16[2048,1024]{1,0:T(8,128)(2,1)} %convolution_convert_fusion.kv_ref), custom_call_target="tpu_custom_call" | custom-call | tf_op jit(solution)/shard_map/attend_forward/pallas_call | solution.py:114
  209.1 3.6 fusion.23
  216.0 3.5 convolution_convert_fusion.15.q_ref
  219.5 22.3 %attend_forward.2 = (bf16[1024,512]{1,0:T(8,128)(2,1)}, f32[4,2,1024]{2,1,0:T(2,128)}) custom-call(s32[27]{0:T(128)} %pad_add_fusion.meta_ref, bf16[1024,512]{1,0:T(8,128)(2,1)} %convolution_convert_fusion.15.q_ref, bf16[2048,1024]{1,0:T(8,128)(2,1)} %convolution_convert_fusion.1.kv_ref), custom_call_target="tpu_custom_call" | custom-call | tf_op jit(solution)/shard_map/attend_forward/pallas_call | solution.py:114
  244.7 4.7 multiply_reduce_fusion.2
  251.8 9.5 %all-gather.6.cloned.1.call-done = bf16[2048,2816]{1,0:T(8,128)(2,1)} async-done(((bf16[64,2816]{1,0:T(8,128)(2,1)}), bf16[2048,2816]{1,0:T(8,128)(2,1)}) %all-gather.6.cloned.1.call-update) | async-done | bytes 11534352 | tf_op jit(solution)/shard_map/all_gather | solution.py:319
  261.3 5.5 fusion.43
  266.8 10.9 %multiply_convert_fusion.3 = (bf16[1024,1408]{1,0:T(8,128)(2,1)}, bf16[1024,1408]{1,0:T(8,128)(2,1)S(1)}, bf16[1024,1408]{1,0:T(8,128)(2,1)}) fusion(f32[1024,1408]{1,0:T(8,128)} %fusion.37, f32[1024,1408]{1,0:T(8,128)S(1)} %fusion.43, bf16[1024,1024]{0,1:T(8,128)(2,1)S(1)} %multiply_convert_fusion.6, bf16[2048,2816]{1,0:T(8,128)(2,1)} %all-gather.6.cloned.1.call-done), kind=kOutput, calls=%fused_computation.17 | convolution fusion | flops 2974416896 | bytes 25165824 | tf_op jit(solution)/shard_map/dot_general | solution.py:26
  279.3 3.6 convolution_convert_fusion.5
  282.9 5.3 fusion.31
  288.3 10.0 %multiply_convert_fusion.1 = (bf16[1024,1408]{1,0:T(8,128)(2,1)}, bf16[1024,1408]{1,0:T(8,128)(2,1)S(1)}, bf16[1024,1408]{1,0:T(8,128)(2,1)}) fusion(f32[1024,1408]{1,0:T(8,128)S(1)} %bitcast.109, f32[1024,1408]{1,0:T(8,128)S(1)} %fusion.31, bf16[1024,1024]{0,1:T(8,128)(2,1)S(1)} %multiply_convert_fusion.6, bf16[2048,2816]{1,0:T(8,128)(2,1)} %all-gather.6.cloned.1.call-done), kind=kOutput, calls=%fused_computation.15 | convolution fusion | flops 2974416896 | bytes 25165824 | tf_op jit(solution)/shard_map/dot_general | solution.py:26
  298.3 3.6 convolution_convert_fusion.4
  305.0 5.8 convolution_convert_fusion.7
  310.9 3.6 convolution_convert_fusion.6
  320.5 6.5 fusion.19
  327.1 3.8 fusion.20
  333.9 6.3 fusion.41
  340.2 7.5 fusion.33
  347.7 5.0 fusion.29
  352.7 6.9 add_add_fusion.1
  359.7 7.7 fusion.27
  367.5 8.6 fusion.16
  377.1 4.3 convolution_convert_fusion.13.do_ref
  381.4 43.0 %attend_backward.2 = (bf16[1024,512]{1,0:T(8,128)(2,1)}, bf16[2048,1024]{1,0:T(8,128)(2,1)}) custom-call(s32[27]{0:T(128)} %pad_add_fusion.meta_ref, bf16[1024,512]{1,0:T(8,128)(2,1)} %convolution_convert_fusion.15.q_ref, bf16[2048,1024]{1,0:T(8,128)(2,1)} %convolution_convert_fusion.1.kv_ref, bf16[1024,512]{1,0:T(8,128)(2,1)} %get-tuple-element.21.o_ref, ...), custom_call_target="tpu_custom_call" | custom-call | tf_op jit(solution)/shard_map/attend_backward/pallas_call | solution.py:226
  424.4 3.6 fusion.89
  433.9 4.1 convolution_convert_fusion.12.do_ref
  438.0 42.8 %attend_backward.3 = (bf16[1024,512]{1,0:T(8,128)(2,1)}, bf16[2048,1024]{1,0:T(8,128)(2,1)}) custom-call(s32[27]{0:T(128)} %pad_add_fusion.meta_ref, bf16[1024,512]{1,0:T(8,128)(2,1)} %convolution_convert_fusion.14.q_ref, bf16[2048,1024]{1,0:T(8,128)(2,1)} %convolution_convert_fusion.kv_ref, bf16[1024,512]{1,0:T(8,128)(2,1)} %get-tuple-element.22.o_ref, ...), custom_call_target="tpu_custom_call" | custom-call | tf_op jit(solution)/shard_map/attend_backward/pallas_call | solution.py:226
  480.8 3.7 fusion.90
  490.5 4.6 fusion.66
  497.2 4.5 fusion.72
  504.2 4.4 fusion.53
  514.8 4.9 fusion.14
  527.8 4.0 fusion.54
  539.1 5.8 pad_maximum_fusion
  544.9 9.7 %copy.259 = bf16[2048,1664]{1,0:T(8,128)(2,1)} copy(bf16[2048,1664]{0,1:T(8,128)(2,1)} %pad_maximum_fusion) | data formatting | bytes 13631488
  558.0 43.1 %all_gather.15 = f32[256,128]{1,0:T(8,128)S(1)} all-gather(f32[8,128]{1,0:T(8,128)S(1)} %broadcast_in_dim.28), channel_id=1, replica_groups=mesh['dp'=16,'tensor'=2] {'tensor','dp'}, dimensions={0}, use_global_device_ids=true | all-gather | bytes 135168 | tf_op jit(solution)/shard_map/all_gather | solution.py:392
  601.7 3.9 copy.244
  606.8 7.8 fusion.13
  614.7 5.4 copy.245
  623.4 113.6 %reduce-scatter.11.cloned.1.call-done = bf16[64,1408]{1,0:T(8,128)(2,1)} async-done(((bf16[2048,1408]{1,0:T(8,128)(2,1)}), bf16[64,1408]{1,0:T(8,128)(2,1)}) %reduce-scatter.11.cloned.1.call-update) | async-done | bytes 180240 | tf_op jit(solution)/shard_map/reduce_scatter | solution.py:268
  738.7 143.9 %reduce-scatter.13.cloned.1.call-done = bf16[64,1664]{1,0:T(8,128)(2,1)} async-done(((bf16[2048,1664]{1,0:T(8,128)(2,1)}), bf16[64,1664]{1,0:T(8,128)(2,1)}) %reduce-scatter.13.cloned.1.call-update) | async-done | bytes 213008
  (247 shorter events, 99.4 us)
Async XLA Ops:
  7.2 17.3 %copy-start.45 = (s32[1,13]{1,0:T(1,128)S(1)}, s32[1,13]{1,0:T(1,128)}, u32[]{:S(2)}) copy-start(s32[1,13]{1,0:T(1,128)} %param.26) | copy-start | bytes 160
  7.2 17.2 %copy-start.46 = (s32[1,13]{1,0:T(1,128)S(1)}, s32[1,13]{1,0:T(1,128)}, u32[]{:S(2)}) copy-start(s32[1,13]{1,0:T(1,128)} %param.25) | copy-start | bytes 160
  7.2 78.3 %all-gather.8.cloned.1.call-start = ((), (), s32[]{:S(2)}) async-start(), calls=%async_computation.6 | async-start | bytes 5947392 | tf_op jit(solution)/shard_map/all_gather | solution.py:322
  7.9 160.8 %all-gather.4.cloned.1.call-start = ((), (), s32[]{:S(2)}) async-start(), calls=%async_computation.4 | async-start | bytes 7028736 | tf_op jit(solution)/shard_map/all_gather | solution.py:318
  13.5 247.8 %all-gather.6.cloned.1.call-start = ((), (), s32[]{:S(2)}) async-start(), calls=%async_computation.5 | async-start | bytes 11894784 | tf_op jit(solution)/shard_map/all_gather | solution.py:319
  15.3 604.7 %reduce-scatter.9.cloned.1.call-start = ((), (), s32[]{:S(2)}) async-start(), calls=%async_computation.8 | async-start | bytes 5947392 | tf_op jit(solution)/shard_map/reduce_scatter | solution.py:268
  18.2 226.4 %copy-start = (bf16[1024,1024]{0,1:T(8,128)(2,1)}, bf16[1024,1024]{0,1:T(8,128)(2,1)S(1)}, u32[]{:S(2)}) copy-start(bf16[1024,1024]{0,1:T(8,128)(2,1)S(1)} %copy.215) | copy-start | bytes 6291460
  18.2 66.2 %collective-permute-start = (bf16[1024,1024]{0,1:T(8,128)(2,1)S(1)}, bf16[1024,1024]{0,1:T(8,128)(2,1)}, u32[]{:S(2)}, u32[]{:S(2)}) collective-permute-start(bf16[1024,1024]{0,1:T(8,128)(2,1)S(1)} %copy.215), channel_id=1, source_target_pairs={{0,1},{2,3},{4,5},{6,7},{8,9},{10,11},{12,13},{14,15},{16,17},{18,... | collective-permute-start | bytes 6291464 | tf_op jit(solution)/shard_map/ppermute | solution.py:304
  85.5 89.9 %copy-start.43 = (f32[1024]{0:T(1024)}, f32[1024]{0:T(1024)S(1)}, u32[]{:S(2)}) copy-start(f32[1024]{0:T(1024)S(1)} %add_rsqrt_fusion.2) | copy-start | bytes 12292
  85.5 8.6 copy-start.31
  85.6 8.6 copy-start.47
  171.3 5.2 copy-start.41
  173.7 5.7 copy-start.27
  175.3 37.4 %copy-start.29 = (bf16[256,1024]{1,0:T(8,128)(2,1)}, bf16[256,1024]{1,0:T(8,128)(2,1)S(1)}, u32[]{:S(2)}) copy-start(bf16[256,1024]{1,0:T(8,128)(2,1)S(1)} %reshape.121) | copy-start | bytes 1572868
  176.6 6.2 copy-start.20
  261.3 27.0 %slice-start.3 = ((s8[5767168]{0:T(1024)(128)(4,1)}), s8[4194304]{0:T(1024)(128)(4,1)S(1)}, s32[]{:S(2)}) async-start(s8[5767168]{0:T(1024)(128)(4,1)} %bitcast.108), calls=%async_computation.14 | async-start | bytes 8388608
  266.8 21.5 %slice-start.4 = ((s8[5767168]{0:T(1024)(128)(4,1)}), s8[1572864]{0:T(1024)(128)(4,1)S(1)}, s32[]{:S(2)}) async-start(s8[5767168]{0:T(1024)(128)(4,1)} %bitcast.108), calls=%async_computation.15 | async-start | bytes 3145728
  305.0 316.7 %reduce-scatter.7.cloned.1.call-start = ((), (), s32[]{:S(2)}) async-start(), calls=%async_computation.7 | async-start | bytes 5947392 | tf_op jit(solution)/shard_map/reduce_scatter | solution.py:268
  305.0 5.8 copy-start.55
  317.4 419.6 %reduce-scatter.11.cloned.1.call-start = ((), (), s32[]{:S(2)}) async-start(), calls=%async_computation.9 | async-start | bytes 5947392 | tf_op jit(solution)/shard_map/reduce_scatter | solution.py:268
  320.3 55.7 %copy-start.6 = (bf16[1024,1024]{0,1:T(8,128)(2,1)}, bf16[1024,1024]{0,1:T(8,128)(2,1)S(1)}, u32[]{:S(2)}) copy-start(bf16[1024,1024]{0,1:T(8,128)(2,1)S(1)} %copy.226) | copy-start | bytes 6291460
  320.5 6.5 copy-start.32
  320.5 6.5 copy-start.51
  333.8 548.8 %reduce-scatter.13.cloned.1.call-start = ((), (), s32[]{:S(2)}) async-start(), calls=%async_computation.10 | async-start | bytes 7028736
  333.8 6.4 copy-start.56
  333.8 13.9 %slice-start = ((s8[11534336]{0:T(1024)(128)(4,1)}), s8[4194304]{0:T(1024)(128)(4,1)S(1)}, s32[]{:S(2)}) async-start(s8[11534336]{0:T(1024)(128)(4,1)} %bitcast.106), calls=%async_computation.11 | async-start | bytes 8388608
  333.9 13.9 %slice-start.1 = ((s8[11534336]{0:T(1024)(128)(4,1)}), s8[4194304]{0:T(1024)(128)(4,1)S(1)}, s32[]{:S(2)}) async-start(s8[11534336]{0:T(1024)(128)(4,1)} %bitcast.106), calls=%async_computation.12 | async-start | bytes 8388608
  340.2 7.5 slice-start.2
  340.2 7.5 copy-start.54
  359.7 16.4 %copy-start.7 = (f32[1024,1024]{0,1:T(8,128)}, f32[1024,1024]{0,1:T(8,128)S(1)}, u32[]{:S(2)}) copy-start(f32[1024,1024]{0,1:T(8,128)S(1)} %add_add_fusion.1) | copy-start | bytes 12582916
  359.7 7.8 copy-start.3
  359.7 7.8 copy-start.9
  359.7 7.8 copy-start.50
  381.4 43.0 %copy-start.30 = (bf16[256,1024]{1,0:T(8,128)(2,1)S(1)}, bf16[256,1024]{1,0:T(8,128)(2,1)}, u32[]{:S(2)}) copy-start(bf16[256,1024]{1,0:T(8,128)(2,1)} %copy-done.29) | copy-start | bytes 1572868
  424.4 5.0 copy-start.19
  424.4 5.0 copy-start.49
  428.1 80.4 %collective-permute-start.1 = (bf16[1024,256]{1,0:T(8,128)(2,1)S(1)}, bf16[1024,256]{1,0:T(8,128)(2,1)}, u32[]{:S(2)}, u32[]{:S(2)}) collective-permute-start(bf16[1024,256]{1,0:T(8,128)(2,1)S(1)} %slice.251), channel_id=1, source_target_pairs={{1,0},{3,2},{5,4},{7,6},{9,8},{11,10},{13,12},{15,14},{17,16},{19,... | collective-permute-start | bytes 1572872 | tf_op jit(solution)/shard_map/ppermute | solution.py:425
  438.0 42.8 %copy-start.28 = (bf16[256,1024]{1,0:T(8,128)(2,1)S(1)}, bf16[256,1024]{1,0:T(8,128)(2,1)}, u32[]{:S(2)}) copy-start(bf16[256,1024]{1,0:T(8,128)(2,1)} %copy-done.27) | copy-start | bytes 1572868
  480.8 7.4 copy-start.22
  480.8 7.4 copy-start.37
  485.8 4.7 copy-start.38
  486.7 23.1 %collective-permute-start.2 = (bf16[1024,256]{1,0:T(8,128)(2,1)}, bf16[1024,256]{1,0:T(8,128)(2,1)}, u32[]{:S(2)}, u32[]{:S(2)}) collective-permute-start(bf16[1024,256]{1,0:T(8,128)(2,1)} %slice.250), channel_id=1, source_target_pairs={{1,0},{3,2},{5,4},{7,6},{9,8},{11,10},{13,12},{15,14},{17,16},{19,... | collective-permute-start | bytes 1572872 | tf_op jit(solution)/shard_map/ppermute | solution.py:425
  490.5 4.7 copy-start.48
  504.2 5.6 copy-start.15
  519.7 8.0 copy-start.8
  527.8 4.9 copy-start.39
  527.8 5.6 copy-start.23
  527.8 5.6 copy-start.36
  (24 other events, 70.8 us)
Sparse Core Ops, SparseCore 0:
  10.9 74.0 all-gather.7
  88.4 80.3 all-gather.3
  172.2 89.0 all-gather.5
  305.1 143.8 reduce-scatter.8
  451.1 142.6 reduce-scatter.6
  595.9 141.0 reduce-scatter.10
  739.3 143.1 reduce-scatter.12

commit v2 on v1

--- a/solution.py
+++ b/solution.py
@@ -264,10 +264,18 @@
     return both.reshape(rows, 2 * width)
 
 
-def scatter(parts):
-    return lax.psum_scatter(
-        jnp.concatenate(parts, axis=0), GATHER_AXES, scatter_dimension=0, tiled=True
-    )
+def swap_sides(array):
+    return lax.ppermute(array, "tensor", [(0, 1), (1, 0)])
+
+
+def all_sum(array):
+    array = array + swap_sides(array)
+    size = lax.axis_size("dp")
+    step = 1
+    while step < size:
+        array = array + lax.ppermute(array, "dp", [(i, i ^ step) for i in range(size)])
+        step *= 2
+    return array
 
 
 def local(
@@ -316,34 +324,32 @@
         axis=1,
     )
     attn_all = lax.all_gather(attn_pack, GATHER_AXES, axis=0, tiled=True)
-    gate_up_all = lax.all_gather(
-        jnp.concatenate([w_gate, w_up], axis=1), GATHER_AXES, axis=0, tiled=True
-    )
-    down_all = lax.all_gather(w_down.T, GATHER_AXES, axis=0, tiled=True)
-
-    def part_of(gathered, t, first, size):
-        return lax.slice(
-            gathered, (t * model_width, first), ((t + 1) * model_width, first + size)
-        )
+    ffn_pack = jnp.concatenate([w_gate, w_up, w_down.T], axis=1)
+    ffn_all = lax.all_gather(ffn_pack, GATHER_AXES, axis=0, tiled=True)
+
+    owners = [1 - side, side]
+
+    def half_of(gathered, u, first, size):
+        return lax.dynamic_slice(gathered, (owners[u] * model_width, first), (model_width, size))
 
     first_latent = query_len
     first_out = first_latent + latent_len
     first_kv = first_out + query_len
     first_gain = first_kv + kv_cols
-    query_w = [part_of(attn_all, t, 0, query_len) for t in range(sides)]
-    latent_w = [part_of(attn_all, t, first_latent, latent_len) for t in range(sides)]
-    out_w = [part_of(attn_all, t, first_out, query_len) for t in range(sides)]
+    query_w = [half_of(attn_all, u, 0, query_len) for u in range(2)]
+    latent_w = [half_of(attn_all, u, first_latent, latent_len) for u in range(2)]
+    out_w = [half_of(attn_all, u, first_out, query_len) for u in range(2)]
     kv_w = [
-        part_of(attn_all, t, first_kv, kv_cols).reshape(dp_size * kv_rows, 2 * kv_len)
-        for t in range(sides)
+        half_of(attn_all, u, first_kv, kv_cols).reshape(dp_size * kv_rows, 2 * kv_len)
+        for u in range(2)
     ]
     gains = attn_all[:, first_gain : first_gain + 2 * gain_len]
     gains = gains.reshape(sides, dp_size, shard_rows, 2, gain_len)[:, :, 0]
     gains = gains.transpose(2, 1, 0, 3).reshape(2, model_width).astype(jnp.float32)
     gain_one, gain_two = gains[0], gains[1]
-    gate_w = [part_of(gate_up_all, t, 0, hidden_len) for t in range(sides)]
-    up_w = [part_of(gate_up_all, t, hidden_len, hidden_len) for t in range(sides)]
-    down_w = [part_of(down_all, t, 0, hidden_len) for t in range(sides)]
+    gate_w = [half_of(ffn_all, u, 0, hidden_len) for u in range(2)]
+    up_w = [half_of(ffn_all, u, hidden_len, hidden_len) for u in range(2)]
+    down_w = [half_of(ffn_all, u, 2 * hidden_len, hidden_len) for u in range(2)]
 
     context_input = jnp.where(side == 0, layer_input, sent)
     inputs = layer_input.astype(jnp.float32)
@@ -352,26 +358,39 @@
     context_in = (norm_stats(context_input.astype(jnp.float32))[0] * gain_one).astype(bf16)
     both_in = jnp.concatenate([context_in, attn_in], axis=0)
     queries, latents, kvs, heads, lses = [], [], [], [], []
-    for t in range(sides):
-        latents.append(mm(both_in, latent_w[t]).astype(bf16))
-        queries.append(mm(attn_in, query_w[t]).astype(bf16))
-        kvs.append(mm(latents[t], kv_w[t]).astype(bf16))
-        out, lse = attend_forward(meta, queries[t], kvs[t])
+    for u in range(2):
+        latents.append(mm(both_in, latent_w[u]).astype(bf16))
+        queries.append(mm(attn_in, query_w[u]).astype(bf16))
+        kvs.append(mm(latents[u], kv_w[u]).astype(bf16))
+        out, lse = attend_forward(meta, queries[u], kvs[u])
         heads.append(out)
         lses.append(lse)
-    branch = sum(mm(heads[t], out_w[t], NT) for t in range(sides))
+    branch = mm(heads[0], out_w[0], NT) + mm(heads[1], out_w[1], NT)
     residual = inputs + branch
     normed_two, inverse_two = norm_stats(residual)
     ffn_in = (normed_two * gain_two).astype(bf16)
 
-    gates = [mm(ffn_in, gate_w[t]) for t in range(sides)]
-    ups = [mm(ffn_in, up_w[t]) for t in range(sides)]
+    def half_grad(left, rights):
+        received = swap_sides(mm(left, rights[0], TN).astype(bf16))
+        return lambda: (mm(left, rights[1], TN) + received.astype(jnp.float32)).astype(bf16)
+
+    gates = [mm(ffn_in, gate_w[u]) for u in range(2)]
+    ups = [mm(ffn_in, up_w[u]) for u in range(2)]
     sigs = [jax.nn.sigmoid(gate) for gate in gates]
-    hiddens = [(gates[t] * sigs[t] * ups[t]).astype(bf16) for t in range(sides)]
-    ffn_out = sum(mm(hiddens[t], down_w[t], NT) for t in range(sides))
+    hiddens = [(gates[u] * sigs[u] * ups[u]).astype(bf16) for u in range(2)]
+
+    first_cols = [0, hidden_len, 2 * hidden_len, 3 * hidden_len]
+    first_pack = jnp.zeros((sides * model_width, 3 * hidden_len + query_len), bf16)
+
+    def put(pack, k, u, value):
+        return lax.dynamic_update_slice(
+            pack, value.astype(bf16), (owners[u] * model_width, first_cols[k])
+        )
+
+    for u in range(2):
+        first_pack = put(first_pack, 0, u, mm(upstream_grad, hiddens[u], TN))
+    ffn_out = mm(hiddens[0], down_w[0], NT) + mm(hiddens[1], down_w[1], NT)
     final_out = (residual + ffn_out).astype(bf16)
-    down_grads = [mm(upstream_grad, hiddens[t], TN).astype(bf16) for t in range(sides)]
-    down_sum = scatter(down_grads)
 
     position = side * row_count + lax.broadcasted_iota(jnp.int32, (row_count, NSEG), 0)
     seg_ids = lax.broadcasted_iota(jnp.int32, (row_count, NSEG), 1)
@@ -388,81 +407,99 @@
             jnp.sum(valid),
         ]
     )
-    stat_rows = jnp.broadcast_to(jnp.pad(stat_terms, (0, 2 * E - 4))[None, :], (8, 2 * E))
-    stat_all = lax.all_gather(stat_rows, GATHER_AXES, axis=0, tiled=True)
-    stat_totals = jnp.sum(stat_all.reshape(sides * dp_size, 8, 2 * E)[:, 0, :4], axis=0)
-    rms_stats = jnp.sqrt(stat_totals[:3] / (stat_totals[3] * model_width))
-
-    ffn_grads = []
+
     normed_grad_two = 0.0
-    for t in range(sides):
-        hidden_grad = mm(upstream_grad, down_w[t])
-        gate_act = gates[t] * sigs[t]
+    for u in range(2):
+        hidden_grad = mm(upstream_grad, down_w[u])
+        gate_act = gates[u] * sigs[u]
         gate_grad = (
-            hidden_grad * ups[t] * sigs[t] * (1.0 + gates[t] * (1.0 - sigs[t]))
+            hidden_grad * ups[u] * sigs[u] * (1.0 + gates[u] * (1.0 - sigs[u]))
         ).astype(bf16)
         up_grad = (hidden_grad * gate_act).astype(bf16)
         normed_grad_two = (
-            normed_grad_two + mm(gate_grad, gate_w[t], NT) + mm(up_grad, up_w[t], NT)
+            normed_grad_two + mm(gate_grad, gate_w[u], NT) + mm(up_grad, up_w[u], NT)
         )
-        ffn_grads.append((mm(ffn_in, gate_grad, TN).astype(bf16), mm(ffn_in, up_grad, TN).astype(bf16)))
-    gate_sum = scatter([pair[0] for pair in ffn_grads])
-    up_sum = scatter([pair[1] for pair in ffn_grads])
+        first_pack = put(first_pack, 1, u, mm(ffn_in, gate_grad, TN))
+        first_pack = put(first_pack, 2, u, mm(ffn_in, up_grad, TN))
     residual_part, gain_two_grad = norm_back(normed_grad_two, gain_two, normed_two, inverse_two)
     residual_grad = upstream_grad.astype(jnp.float32) + residual_part
     branch_grad = residual_grad.astype(bf16)
-
-    attn_grads = []
-    normed_grad_one = 0.0
-    for t in range(sides):
-        out_grad = mm(branch_grad, heads[t], TN).astype(bf16)
-        heads_grad = mm(branch_grad, out_w[t]).astype(bf16)
+    for u in range(2):
+        first_pack = put(first_pack, 3, u, mm(branch_grad, heads[u], TN))
+    first_pack, branch_grad = lax.optimization_barrier((first_pack, branch_grad))
+    ffn_sum = lax.psum_scatter(first_pack, GATHER_AXES, scatter_dimension=0, tiled=True)
+
+    query_grads, kv_grads, latent_parts = [], [], []
+    for u in range(2):
+        heads_grad = mm(branch_grad, out_w[u]).astype(bf16)
+        if u == 1:
+            query_out = mm(attn_in, query_grads[0], TN).astype(bf16)
+            kv_out = mm(latents[0], kv_grads[0], TN).astype(bf16)
+            query_out, kv_out, heads_grad = lax.optimization_barrier(
+                (query_out, kv_out, heads_grad)
+            )
+            query_in = swap_sides(query_out)
+            kv_in = swap_sides(kv_out)
         query_grad, kv_grad = attend_backward(
-            meta, queries[t], kvs[t], heads[t], heads_grad, lses[t]
+            meta, queries[u], kvs[u], heads[u], heads_grad, lses[u]
         )
-        latent_part = mm(kv_grad, kv_w[t], NT)
-        context_part = latent_part[:row_count]
-        returned = lax.ppermute(context_part.astype(bf16), "tensor", [(1, 0)])
-        kv_w_grad = mm(latents[t], kv_grad, TN).astype(bf16)
-        query_w_grad = mm(attn_in, query_grad, TN).astype(bf16)
-        latent_grad = (
-            latent_part[row_count:]
-            + jnp.where(side == 0, context_part, 0.0)
-            + returned.astype(jnp.float32)
-        ).astype(bf16)
-        latent_w_grad = mm(attn_in, latent_grad, TN).astype(bf16)
-        normed_grad_one = (
-            normed_grad_one + mm(query_grad, query_w[t], NT) + mm(latent_grad, latent_w[t], NT)
+        query_grads.append(query_grad)
+        kv_grads.append(kv_grad)
+        latent_parts.append(mm(kv_grad, kv_w[u], NT))
+    query_half = (mm(attn_in, query_grads[1], TN) + query_in.astype(jnp.float32)).astype(bf16)
+    kv_half = (mm(latents[1], kv_grads[1], TN) + kv_in.astype(jnp.float32)).astype(bf16)
+    latent_grads = []
+    for u in range(2):
+        returned = lax.ppermute(
+            latent_parts[1 - u][:row_count].astype(bf16), "tensor", [(1, 0)]
         )
-        attn_grads.append(
-            [query_w_grad, latent_w_grad, out_grad, kv_w_grad.reshape(model_width, kv_cols)]
+        latent_grads.append(
+            (
+                latent_parts[u][row_count:]
+                + jnp.where(side == 0, latent_parts[u][:row_count], 0.0)
+                + returned.astype(jnp.float32)
+            ).astype(bf16)
         )
+    latent_half = half_grad(attn_in, latent_grads)
+    attn_pack = jnp.concatenate(
+        [query_half, latent_half(), kv_half.reshape(model_width, kv_cols)], axis=1
+    )
+    attn_pack, ffn_sum = lax.optimization_barrier((attn_pack, ffn_sum))
+    attn_sum = lax.psum_scatter(attn_pack, "dp", scatter_dimension=0, tiled=True)
+    attn_sum = attn_sum.astype(jnp.float32)
+    normed_grad_one = (
+        mm(query_grads[0], query_w[0], NT)
+        + mm(query_grads[1], query_w[1], NT)
+        + mm(latent_grads[0], latent_w[0], NT)
+        + mm(latent_grads[1], latent_w[1], NT)
+    )
     input_part, gain_one_grad = norm_back(normed_grad_one, gain_one, normed_one, inverse_one)
     input_grad = residual_grad + input_part
 
-    gain_grads = jnp.stack([gain_one_grad, gain_two_grad]).reshape(2, dp_size, sides, gain_len)
-    gain_grads = gain_grads.transpose(2, 1, 0, 3).reshape(sides, dp_size, 1, 2 * gain_len)
-    gain_grads = jnp.pad(
-        gain_grads.astype(bf16),
-        ((0, 0), (0, 0), (0, shard_rows - 1), (0, gain_cols - 2 * gain_len)),
-    ).reshape(sides, model_width, gain_cols)
-    attn_sum = scatter(
-        [jnp.concatenate(attn_grads[t] + [gain_grads[t]], axis=1) for t in range(sides)]
-    ).astype(jnp.float32)
-    kv_sum = attn_sum[:, first_kv:first_gain].reshape(kv_rows, kv_len // PAIR, 2, PAIR)
+    stat_row = jnp.pad(stat_terms, (0, 8 * 2 * E - 4))
+    totals = all_sum(
+        jnp.concatenate([gain_one_grad, gain_two_grad, stat_row]).reshape(-1, 2 * E)
+    ).reshape(-1)
+    own_start = lax.axis_index(("dp", "tensor")) * gain_len
+    stat_totals = totals[2 * model_width : 2 * model_width + 4]
+    rms_stats = jnp.sqrt(stat_totals[:3] / (stat_totals[3] * model_width))
+    kv_sum = attn_sum[:, first_out : first_out + kv_cols].reshape(
+        kv_rows, kv_len // PAIR, 2, PAIR
+    )
+    ffn_sum = ffn_sum.astype(jnp.float32)
     return (
         final_out,
         input_grad,
-        attn_sum[0, first_gain : first_gain + gain_len],
+        lax.dynamic_slice_in_dim(totals, own_start, gain_len),
         attn_sum[:, :query_len],
         attn_sum[:, first_latent:first_out],
         kv_sum[:, :, 0].reshape(1, kv_rows, kv_len),
         kv_sum[:, :, 1].reshape(1, kv_rows, kv_len),
-        attn_sum[:, first_out:first_kv].T,
-        attn_sum[0, first_gain + gain_len : first_gain + 2 * gain_len],
-        gate_sum.astype(jnp.float32),
-        up_sum.astype(jnp.float32),
-        down_sum.astype(jnp.float32).T,
+        ffn_sum[:, 3 * hidden_len :].T,
+        lax.dynamic_slice_in_dim(totals, model_width + own_start, gain_len),
+        ffn_sum[:, hidden_len : 2 * hidden_len],
+        ffn_sum[:, 2 * hidden_len : 3 * hidden_len],
+        ffn_sum[:, :hidden_len].T,
         rms_stats,
     )
 

time: 901 us -> 661 us (0.73)
  waiting for transfers between devices: 396 us -> 194 us
  blocking collectives: 43.1 us -> 0 us
  starting transfers between devices: 9.25 us -> 31.4 us
  other arithmetic: 41.1 us -> 23.5 us
  Pallas kernels: 131 us -> 142 us
  matrix products: 196 us -> 186 us
    unnamed x8 -> x4, waiting for transfers between devices: 145 us -> 0.07 us
    all_gather x1, waiting for transfers between devices: 69.2 us -> 8.23 us  [local(): attn_all = lax.all_gather(attn_pack, GATHER_AXES, axis=0, tiled=True)]
    reduce_scatter x3 -> x2, waiting for transfers between devices: 114 us -> 62.7 us  [the longest x1 32.8 us: local(): lax.psum_scatter(first_pack, GATHER_AXES, scatter_dimension=0, tiled=True)]
    all_gather x1 -> x0, blocking collectives: 43.1 us -> none  [local(): stat_all = lax.all_gather(stat_rows, GATHER_AXES, axis=0, tiled=True)]
    ppermute x2 -> x10, waiting for transfers between devices: 0.01 us -> 37.9 us  [the longest x4 28.8 us: swap_sides(): return lax.ppermute(array, 'tensor', [(0, 1), (1, 0)])]
    ppermute x2 -> x10, starting transfers between devices: 2.78 us -> 25 us  [the longest x4 16.4 us: all_sum(): lax.ppermute(array, 'dp', [(i, i ^ step) for i in range(size)])]
    all_gather x2 -> x1, waiting for transfers between devices: 9.56 us -> 31.4 us  [local(): ffn_all = lax.all_gather(ffn_pack, GATHER_AXES, axis=0, tiled=True)]
    pallas_call x2, Pallas kernels: 45 us -> 56.1 us  [attend_forward(): pl.pallas_call(forward_kernel, grid_spec=pltpu.PrefetchScalarGridSpec(num...]
  transfers between devices with their start and end apart: 10 -> 15, of which waited for: 5 -> 9; matrix products, arithmetic and copies ran while one was open for 27% -> 18% of each run, Pallas kernels for 15% -> 22%
where the time goes in v2:
time: 661 us; the launch traced here: 651 us
  waiting for transfers between devices  194 us (29%)
  matrix products  186 us (28%)
  Pallas kernels  142 us (21%)
  local copies, waits for them, and re-layouts  59.1 us (9%)
  starting transfers between devices  31.4 us (5%)
  other arithmetic  23.5 us (4%)
  between operations  15.5 us (2%)
    dot_general x42, matrix products, mm(): lax.dot_general(left, right, dims, preferred_element_type=jnp.float32)  186 us
    pallas_call x2, Pallas kernels, attend_backward(): pl.pallas_call(backward_kernel, grid_spec=pltpu.PrefetchScalarGridSpec(nu...  85.8 us
    pallas_call x2, Pallas kernels, attend_forward(): pl.pallas_call(forward_kernel, grid_spec=pltpu.PrefetchScalarGridSpec(num...  56.1 us
    ppermute x1, waiting for transfers between devices, local(): sent = lax.ppermute(layer_input, 'tensor', [(0, 1)])  53.9 us
    reduce_scatter x1, waiting for transfers between devices, local(): lax.psum_scatter(first_pack, GATHER_AXES, scatter_dimension=0, tiled=True)  32.8 us
    unnamed x125, local copies, waits for them, and re-layouts  31.9 us
    all_gather x1, waiting for transfers between devices, local(): ffn_all = lax.all_gather(ffn_pack, GATHER_AXES, axis=0, tiled=True)  31.4 us
    reduce_scatter x1, waiting for transfers between devices, local(): lax.psum_scatter(attn_pack, 'dp', scatter_dimension=0, tiled=True)  29.9 us
  transfers between devices with their start and end apart: 15, of which 9 were waited for; matrix products, arithmetic and copies ran while one was open for 18% of the time, Pallas kernels for 22%

profile of v2, /device:TPU:0, one launch (start us, length us, event | category | flops | bytes accessed | tf_op | source)
XLA Modules:
  0.0 651.4 jit_solution(2883490882576036850)
XLA Ops:
  17.7 6.2 collective-permute-start
  25.2 4.0 copy.145
  29.8 53.9 %collective-permute-done = bf16[1024,1024]{0,1:T(8,128)(2,1)} collective-permute-done((bf16[1024,1024]{0,1:T(8,128)(2,1)S(1)}, bf16[1024,1024]{0,1:T(8,128)(2,1)}, u32[]{:S(2)}, u32[]{:S(2)}) %collective-permute-start) | collective-permute-done | bytes 2097184 | tf_op jit(solution)/shard_map/ppermute | solution.py:312
  84.7 8.2 %all-gather.3.cloned.1.call-done = bf16[2048,1664]{1,0:T(8,128)(2,1)} async-done(((bf16[64,1664]{1,0:T(8,128)(2,1)}), bf16[2048,1664]{1,0:T(8,128)(2,1)}) %all-gather.3.cloned.1.call-update) | async-done | bytes 6815760 | tf_op jit(solution)/shard_map/all_gather | solution.py:326
  103.7 3.9 convolution_convert_fusion.14.q_ref
  107.6 3.3 convolution_convert_fusion.1.kv_ref
  110.8 33.3 %attend_forward.2 = (bf16[1024,512]{1,0:T(8,128)(2,1)}, f32[4,2,1024]{2,1,0:T(2,128)}) custom-call(s32[27]{0:T(128)} %pad_add_fusion.meta_ref, bf16[1024,512]{1,0:T(8,128)(2,1)} %convolution_convert_fusion.14.q_ref, bf16[2048,1024]{1,0:T(8,128)(2,1)} %convolution_convert_fusion.1.kv_ref), custom_call_target="tpu_custom_call" | custom-call | tf_op jit(solution)/shard_map/attend_forward/pallas_call | solution.py:114
  144.2 3.8 fusion.36
  148.0 3.9 convolution_convert_fusion.13.q_ref
  155.1 22.8 %attend_forward.3 = (bf16[1024,512]{1,0:T(8,128)(2,1)}, f32[4,2,1024]{2,1,0:T(2,128)}) custom-call(s32[27]{0:T(128)} %pad_add_fusion.meta_ref, bf16[1024,512]{1,0:T(8,128)(2,1)} %convolution_convert_fusion.13.q_ref, bf16[2048,1024]{1,0:T(8,128)(2,1)} %convolution_convert_fusion.kv_ref), custom_call_target="tpu_custom_call" | custom-call | tf_op jit(solution)/shard_map/attend_forward/pallas_call | solution.py:114
  180.5 4.7 multiply_reduce_fusion.2
  187.7 31.4 %all-gather.5.cloned.1.call-done = bf16[2048,4224]{1,0:T(8,128)(2,1)} async-done(((bf16[64,4224]{1,0:T(8,128)(2,1)}), bf16[2048,4224]{1,0:T(8,128)(2,1)}) %all-gather.5.cloned.1.call-update) | async-done | bytes 17301520 | tf_op jit(solution)/shard_map/all_gather | solution.py:328
  219.1 5.3 fusion.59
  224.4 5.4 fusion.55
  229.9 8.8 %fusion.11 = (bf16[1024,1408]{1,0:T(8,128)(2,1)}, bf16[1024,1408]{1,0:T(8,128)(2,1)}, bf16[1024,1408]{1,0:T(8,128)(2,1)S(1)}) fusion(f32[1024,1408]{1,0:T(8,128)S(1)} %fusion.59, f32[1024,1408]{1,0:T(8,128)S(1)} %fusion.55, bf16[1024,1024]{1,0:T(8,128)(2,1)S(1)} %copy-done.30, bf16[2048,4224]{1,0:T(8,128)(2,1)} %all-gather.5.cloned.1.call-done, ...), kind=kOutput, calls=%fused_computation.21 | convolution fusion | flops 2974416896 | bytes 25165828 | tf_op jit(solution)/shard_map/dot_general | solution.py:26
  240.3 5.0 fusion.31
  245.3 3.3 copy.152
  248.6 6.1 fusion.47
  254.7 5.5 fusion.43
  260.2 8.7 %fusion.7 = (bf16[1024,1408]{1,0:T(8,128)(2,1)}, bf16[1024,1408]{1,0:T(8,128)(2,1)}, bf16[1024,1408]{1,0:T(8,128)(2,1)S(1)}) fusion(f32[1024,1408]{1,0:T(8,128)S(1)} %fusion.47, f32[1024,1408]{1,0:T(8,128)S(1)} %fusion.43, bf16[1024,1024]{1,0:T(8,128)(2,1)S(1)} %copy-done.31, bf16[2048,4224]{1,0:T(8,128)(2,1)} %all-gather.5.cloned.1.call-done, s32[]{:T(128)S(6)} %select_n.74), kind=kOutput, calls=%fused_computation.15 | convolution fusion | flops 2974416896 | bytes 25165828 | tf_op jit(solution)/shard_map/dot_general | solution.py:26
  270.5 4.6 fusion.32
  275.2 4.6 copy.153
  285.7 3.7 fusion.30
  289.4 3.7 fusion.29
  293.2 3.7 fusion.28
  296.9 3.7 fusion.27
  300.7 10.4 %fusion.39 = f32[1024,1024]{0,1:T(8,128)S(1)} fusion(bf16[1024,1408]{1,0:T(8,128)(2,1)} %copy-done.57, bf16[2048,4224]{1,0:T(8,128)(2,1)} %all-gather.5.cloned.1.call-done, s32[]{:T(128)S(6)} %select_n.74), kind=kOutput, calls=%fused_computation.72 | convolution fusion | flops 2952790016 | bytes 9961476 | tf_op jit(solution)/shard_map/dot_general | solution.py:26
  311.1 6.9 %fusion.41 = f32[1024,1024]{0,1:T(8,128)} fusion(bf16[1024,1408]{1,0:T(8,128)(2,1)S(1)} %copy-done.56, bf16[2048,4224]{1,0:T(8,128)(2,1)} %all-gather.5.cloned.1.call-done, s32[]{:T(128)S(6)} %select_n.74), kind=kOutput, calls=%fused_computation.74 | convolution fusion | flops 2952790016 | bytes 9961476 | tf_op jit(solution)/shard_map/dot_general | solution.py:26
  318.0 6.9 %fusion.45 = f32[1024,1024]{0,1:T(8,128)} fusion(bf16[1024,1408]{1,0:T(8,128)(2,1)S(1)} %copy-done.55, bf16[2048,4224]{1,0:T(8,128)(2,1)} %all-gather.5.cloned.1.call-done, s32[]{:T(128)S(6)} %select_n.74), kind=kOutput, calls=%fused_computation.78 | convolution fusion | flops 2952790016 | bytes 9961476 | tf_op jit(solution)/shard_map/dot_general | solution.py:26
  324.9 7.0 %fusion.53 = f32[1024,1024]{0,1:T(8,128)} fusion(bf16[1024,1408]{1,0:T(8,128)(2,1)S(1)} %copy-done.54, bf16[2048,4224]{1,0:T(8,128)(2,1)} %all-gather.5.cloned.1.call-done, s32[]{:T(128)S(6)} %select_n.71), kind=kOutput, calls=%fused_computation.86 | convolution fusion | flops 2952790016 | bytes 9961476 | tf_op jit(solution)/shard_map/dot_general | solution.py:26
  331.9 7.0 %fusion.61 = f32[1024,1024]{0,1:T(8,128)} fusion(f32[1024,1024]{0,1:T(8,128)S(1)} %fusion.39, bf16[1024,1408]{1,0:T(8,128)(2,1)S(1)} %copy-done.53, bf16[2048,4224]{1,0:T(8,128)(2,1)} %all-gather.5.cloned.1.call-done, s32[]{:T(128)S(6)} %select_n.71), kind=kOutput, calls=%fused_computation.98 | convolution fusion | flops 2953838592 | bytes 14155780 | tf_op jit(solution)/shard_map/dot_general | solution.py:26
  338.9 13.4 %multiply_reduce_fusion = (f32[1024]{0:T(1024)S(1)}, f32[1024]{0:T(1024)S(1)}, f32[]{:T(128)}, f32[]{:T(128)}, f32[]{:T(128)}, /*index=5*/bf16[1024,1024]{0,1:T(8,128)(2,1)}, f32[1024,1024]{0,1:T(8,128)S(1)}) fusion(f32[1024,1024]{0,1:T(8,128)S(1)} %copy-done.1, f32[1024]{0:T(1024)S(1)} %add_rsqrt_fusion, f32[1024]{0:T(1024)S(1)} %mul.238, ...), kind=kOutput, calls=%fused_computation.44 | convolution fusion | flops 2973759488 | bytes 37244944 | tf_op jit(solution)/shard_map/dot_general | solution.py:26
  360.6 3.5 convolution_convert_fusion.10.do_ref
  364.1 43.1 %attend_backward.2 = (bf16[1024,512]{1,0:T(8,128)(2,1)}, bf16[2048,1024]{1,0:T(8,128)(2,1)}) custom-call(s32[27]{0:T(128)} %pad_add_fusion.meta_ref, bf16[1024,512]{1,0:T(8,128)(2,1)} %convolution_convert_fusion.14.q_ref, bf16[2048,1024]{1,0:T(8,128)(2,1)} %convolution_convert_fusion.1.kv_ref, bf16[1024,512]{1,0:T(8,128)(2,1)} %get-tuple-element.28.o_ref, ...), custom_call_target="tpu_custom_call" | custom-call | tf_op jit(solution)/shard_map/attend_backward/pallas_call | solution.py:226
  407.2 3.7 convolution_convert_fusion.8.do_ref
  418.7 42.7 %attend_backward.3 = (bf16[1024,512]{1,0:T(8,128)(2,1)}, bf16[2048,1024]{1,0:T(8,128)(2,1)}) custom-call(s32[27]{0:T(128)} %pad_add_fusion.meta_ref, bf16[1024,512]{1,0:T(8,128)(2,1)} %convolution_convert_fusion.13.q_ref, bf16[2048,1024]{1,0:T(8,128)(2,1)} %convolution_convert_fusion.kv_ref, bf16[1024,512]{1,0:T(8,128)(2,1)} %get-tuple-element.29.o_ref, ...), custom_call_target="tpu_custom_call" | custom-call | tf_op jit(solution)/shard_map/attend_backward/pallas_call | solution.py:226
  461.4 3.7 fusion.130
  466.8 3.5 collective-permute-start.10
  478.2 4.5 collective-permute-done.1
  487.8 5.1 fusion.22
  498.4 28.8 %collective-permute-done.9 = bf16[1024,256]{1,0:T(8,128)(2,1)} collective-permute-done((bf16[1024,256]{1,0:T(8,128)(2,1)}, bf16[1024,256]{1,0:T(8,128)(2,1)}, u32[]{:S(2)}, u32[]{:S(2)}) %collective-permute-start.9) | collective-permute-done | bytes 524320 | tf_op jit(solution)/shard_map/ppermute | solution.py:268
  533.8 32.8 %reduce-scatter.3.cloned.1.call-done = bf16[64,4736]{1,0:T(8,128)(2,1)} async-done(((bf16[2048,4736]{1,0:T(8,128)(2,1)}), bf16[64,4736]{1,0:T(8,128)(2,1)}) %reduce-scatter.3.cloned.1.call-update) | async-done | bytes 606224 | tf_op jit(solution)/shard_map/reduce_scatter | solution.py:430
  569.4 14.4 %collective-permute-start.5 = (f32[24,128]{1,0:T(8,128)S(1)}, f32[24,128]{1,0:T(8,128)S(1)}, u32[]{:S(2)}, u32[]{:S(2)}) collective-permute-start(f32[24,128]{1,0:T(8,128)S(1)} %add.208), channel_id=1, source_target_pairs={{0,4},{2,6},{4,0},{6,2},{8,12},{10,14},{12,8},{14,10},{16,20},{18,... | collective-permute-start | bytes 36872 | tf_op jit(solution)/shard_map/ppermute | solution.py:276
  583.9 4.0 copy.160
  587.9 3.7 collective-permute-done.6
  591.6 8.6 %fusion.21 = f32[1024,1024]{0,1:T(8,128)} fusion(bf16[1024,1024]{0,1:T(8,128)(2,1)S(1)} %copy-done.4, f32[1024,1024]{0,1:T(8,128)} %get-tuple-element.142, f32[1024]{0:T(1024)S(1)} %broadcast_multiply_fusion, f32[1024]{0:T(1024)S(1)} %copy-done.42, f32[1024]{0:T(1024)S(1)} %copy-done.44, f32[1024]{0:T(1024)S(1)} %broadcast_multiply_fusion.1, ...), kind=kLoop, calls=%fused_computation.37 | loop fusion | flops 14680064 | bytes 20996096 | tf_op jit(solution)/shard_map/add | solution.py:477
  600.2 5.4 copy.161
  610.4 29.9 %reduce-scatter.5.cloned.1.call-done = bf16[64,1024]{1,0:T(8,128)(2,1)} async-done(((bf16[1024,1024]{1,0:T(8,128)(2,1)}), bf16[64,1024]{1,0:T(8,128)(2,1)}) %reduce-scatter.5.cloned.1.call-update) | async-done | bytes 131088 | tf_op jit(solution)/shard_map/reduce_scatter | solution.py:468
  (225 shorter events, 95.3 us)
Async XLA Ops:
  7.2 16.8 %copy-start.47 = (s32[1,13]{1,0:T(1,128)S(1)}, s32[1,13]{1,0:T(1,128)}, u32[]{:S(2)}) copy-start(s32[1,13]{1,0:T(1,128)} %param.26) | copy-start | bytes 160
  7.2 85.8 %all-gather.3.cloned.1.call-start = ((), (), s32[]{:S(2)}) async-start(), calls=%async_computation.2 | async-start | bytes 7028736 | tf_op jit(solution)/shard_map/all_gather | solution.py:326
  12.7 206.4 %all-gather.5.cloned.1.call-start = ((), (), s32[]{:S(2)}) async-start(), calls=%async_computation.3 | async-start | bytes 17842176 | tf_op jit(solution)/shard_map/all_gather | solution.py:328
  14.7 14.5 %copy-start.48 = (s32[1,13]{1,0:T(1,128)S(1)}, s32[1,13]{1,0:T(1,128)}, u32[]{:S(2)}) copy-start(s32[1,13]{1,0:T(1,128)} %param.25) | copy-start | bytes 160
  14.8 551.9 %reduce-scatter.3.cloned.1.call-start = ((), (), s32[]{:S(2)}) async-start(), calls=%async_computation.4 | async-start | bytes 20004864 | tf_op jit(solution)/shard_map/reduce_scatter | solution.py:430
  17.7 162.8 %copy-start.3 = (bf16[1024,1024]{0,1:T(8,128)(2,1)}, bf16[1024,1024]{0,1:T(8,128)(2,1)S(1)}, u32[]{:S(2)}) copy-start(bf16[1024,1024]{0,1:T(8,128)(2,1)S(1)} %copy.134) | copy-start | bytes 6291460
  17.7 66.0 %collective-permute-start = (bf16[1024,1024]{0,1:T(8,128)(2,1)S(1)}, bf16[1024,1024]{0,1:T(8,128)(2,1)}, u32[]{:S(2)}, u32[]{:S(2)}) collective-permute-start(bf16[1024,1024]{0,1:T(8,128)(2,1)S(1)} %copy.134), channel_id=1, source_target_pairs={{0,1},{2,3},{4,5},{6,7},{8,9},{10,11},{12,13},{14,15},{16,17},{18,... | collective-permute-start | bytes 6291464 | tf_op jit(solution)/shard_map/ppermute | solution.py:312
  84.7 16.0 %copy-start.43 = (f32[1024]{0:T(1024)}, f32[1024]{0:T(1024)S(1)}, u32[]{:S(2)}) copy-start(f32[1024]{0:T(1024)S(1)} %add_rsqrt_fusion.2) | copy-start | bytes 12292
  95.5 5.2 copy-start.41
  97.9 9.6 %copy-start.28 = (bf16[256,1024]{1,0:T(8,128)(2,1)}, bf16[256,1024]{1,0:T(8,128)(2,1)S(1)}, u32[]{:S(2)}) copy-start(bf16[256,1024]{1,0:T(8,128)(2,1)S(1)} %reshape.95) | copy-start | bytes 1572868
  99.5 52.4 %copy-start.26 = (bf16[256,1024]{1,0:T(8,128)(2,1)}, bf16[256,1024]{1,0:T(8,128)(2,1)S(1)}, u32[]{:S(2)}) copy-start(bf16[256,1024]{1,0:T(8,128)(2,1)S(1)} %reshape.96) | copy-start | bytes 1572868
  103.7 3.9 copy-start.16
  144.2 3.8 copy-start.19
  148.0 3.9 copy-start.14
  155.1 22.8 %copy-start.10 = (bf16[1024,512]{1,0:T(8,128)(2,1)S(1)}, bf16[1024,512]{1,0:T(8,128)(2,1)}, u32[]{:S(2)}) copy-start(bf16[1024,512]{1,0:T(8,128)(2,1)} %get-tuple-element.28.o_ref) | copy-start | bytes 3145732
  187.7 36.7 %copy-start.32 = (bf16[1024,1024]{0,1:T(8,128)(2,1)}, bf16[1024,1024]{0,1:T(8,128)(2,1)S(1)}, u32[]{:S(2)}) copy-start(bf16[1024,1024]{0,1:T(8,128)(2,1)S(1)} %multiply_convert_fusion.2) | copy-start | bytes 6291460
  224.4 5.5 copy-start.30
  248.6 6.1 copy-start.33
  254.7 5.5 copy-start.31
  285.7 3.7 copy-start.54
  289.4 3.8 copy-start.55
  293.2 3.7 copy-start.56
  300.7 10.4 %copy-start.2 = (bf16[2048,4736]{1,0:T(8,128)(2,1)}, bf16[2048,4736]{1,0:T(8,128)(2,1)S(1)}, u32[]{:S(2)}) copy-start(bf16[2048,4736]{1,0:T(8,128)(2,1)S(1)} %fusion.27) | copy-start | bytes 58195972
  324.9 7.0 %copy-start.53 = (bf16[1024,1408]{1,0:T(8,128)(2,1)S(1)}, bf16[1024,1408]{1,0:T(8,128)(2,1)}, u32[]{:S(2)}) copy-start(bf16[1024,1408]{1,0:T(8,128)(2,1)} %copy-done.52) | copy-start | bytes 8650756
  331.9 7.0 %copy-start.1 = (f32[1024,1024]{0,1:T(8,128)S(1)}, f32[1024,1024]{0,1:T(8,128)}, u32[]{:S(2)}) copy-start(f32[1024,1024]{0,1:T(8,128)} %copy-done) | copy-start | bytes 12582916
  331.9 7.0 %copy-start.40 = (f32[1024]{0:T(1024)S(1)}, f32[1024]{0:T(1024)}, u32[]{:S(2)}) copy-start(f32[1024]{0:T(1024)} %convert_element_type.213) | copy-start | bytes 12292
  338.9 13.5 %copy-start.6 = (bf16[1024,1024]{0,1:T(8,128)(2,1)S(1)}, bf16[1024,1024]{0,1:T(8,128)(2,1)}, u32[]{:S(2)}) copy-start(bf16[1024,1024]{0,1:T(8,128)(2,1)} %copy.145) | copy-start | bytes 6291460
  359.0 281.3 %reduce-scatter.5.cloned.1.call-start = ((), (), s32[]{:S(2)}) async-start(), calls=%async_computation.5 | async-start | bytes 2228224 | tf_op jit(solution)/shard_map/reduce_scatter | solution.py:468
  417.2 44.2 %copy-start.27 = (bf16[256,1024]{1,0:T(8,128)(2,1)S(1)}, bf16[256,1024]{1,0:T(8,128)(2,1)}, u32[]{:S(2)}) copy-start(bf16[256,1024]{1,0:T(8,128)(2,1)} %copy-done.26) | copy-start | bytes 1572868
  417.3 67.2 %collective-permute-start.2 = (bf16[1024,256]{1,0:T(8,128)(2,1)S(1)}, bf16[1024,256]{1,0:T(8,128)(2,1)}, u32[]{:S(2)}, u32[]{:S(2)}) collective-permute-start(bf16[1024,256]{1,0:T(8,128)(2,1)S(1)} %slice.124), channel_id=1, source_target_pairs={{1,0},{3,2},{5,4},{7,6},{9,8},{11,10},{13,12},{15,14},{17,16},{19,... | collective-permute-start | bytes 1572872 | tf_op jit(solution)/shard_map/ppermute | solution.py:453
  461.4 5.4 copy-start.51
  461.4 9.0 %copy-start.38 = (bf16[1024,512]{1,0:T(8,128)(2,1)S(1)}, bf16[1024,512]{1,0:T(8,128)(2,1)}, u32[]{:S(2)}) copy-start(bf16[1024,512]{1,0:T(8,128)(2,1)} %get-tuple-element.32) | copy-start | bytes 3145732
  465.1 10.4 %copy-start.35 = (bf16[1024,512]{1,0:T(8,128)(2,1)S(1)}, bf16[1024,512]{1,0:T(8,128)(2,1)}, u32[]{:S(2)}) copy-start(bf16[1024,512]{1,0:T(8,128)(2,1)} %get-tuple-element.36) | copy-start | bytes 3145732
  465.2 17.6 %collective-permute-start.1 = (bf16[1024,256]{1,0:T(8,128)(2,1)S(1)}, bf16[1024,256]{1,0:T(8,128)(2,1)S(1)}, u32[]{:S(2)}, u32[]{:S(2)}) collective-permute-start(bf16[1024,256]{1,0:T(8,128)(2,1)S(1)} %slice.123), channel_id=1, source_target_pairs={{1,0},{3,2},{5,4},{7,6},{9,8},{11,10},{13,12},{15,14},{17,16},{19,... | collective-permute-start | bytes 1572872 | tf_op jit(solution)/shard_map/ppermute | solution.py:453
  466.8 28.2 %collective-permute-start.10 = (bf16[256,1024]{1,0:T(8,128)(2,1)S(1)}, bf16[256,1024]{1,0:T(8,128)(2,1)S(1)}, u32[]{:S(2)}, u32[]{:S(2)}) collective-permute-start(bf16[256,1024]{1,0:T(8,128)(2,1)S(1)} %copy-done.51), channel_id=1, source_target_pairs={{0,1},{1,0},{2,3},{3,2},{4,5},{5,4},{6,7},{7,6},{8,9},{9,8},{10,11... | collective-permute-start | bytes 1572872 | tf_op jit(solution)/shard_map/ppermute | solution.py:268
  470.3 59.4 %collective-permute-start.8 = (bf16[1024,512]{1,0:T(8,128)(2,1)}, bf16[1024,512]{1,0:T(8,128)(2,1)}, u32[]{:S(2)}, u32[]{:S(2)}) collective-permute-start(bf16[1024,512]{1,0:T(8,128)(2,1)} %convolution_convert_fusion.9), channel_id=1, source_target_pairs={{0,1},{1,0},{2,3},{3,2},{4,5},{5,4},{6,7},{7,6},{8,9},{9,8},{10,11... | collective-permute-start | bytes 3145736 | tf_op jit(solution)/shard_map/ppermute | solution.py:268
  475.5 7.5 %copy-start.21 = (bf16[1024,1024]{0,1:T(8,128)(2,1)S(1)}, bf16[1024,1024]{0,1:T(8,128)(2,1)}, u32[]{:S(2)}) copy-start(bf16[1024,1024]{0,1:T(8,128)(2,1)} %copy-done.18) | copy-start | bytes 6291460
  484.5 42.7 %collective-permute-start.9 = (bf16[1024,256]{1,0:T(8,128)(2,1)}, bf16[1024,256]{1,0:T(8,128)(2,1)}, u32[]{:S(2)}, u32[]{:S(2)}) collective-permute-start(bf16[1024,256]{1,0:T(8,128)(2,1)} %convolution_convert_fusion.15), channel_id=1, source_target_pairs={{0,1},{1,0},{2,3},{3,2},{4,5},{5,4},{6,7},{7,6},{8,9},{9,8},{10,11... | collective-permute-start | bytes 1572872 | tf_op jit(solution)/shard_map/ppermute | solution.py:268
  487.8 7.2 %copy-start.15 = (bf16[2048,256]{1,0:T(8,128)(2,1)S(1)}, bf16[2048,256]{1,0:T(8,128)(2,1)}, u32[]{:S(2)}) copy-start(bf16[2048,256]{1,0:T(8,128)(2,1)} %copy-done.14) | copy-start | bytes 3145732
  487.8 7.1 %copy-start.49 = (bf16[2048,1024]{1,0:T(8,128)(2,1)S(1)}, bf16[2048,1024]{1,0:T(8,128)(2,1)}, u32[]{:S(2)}) copy-start(bf16[2048,1024]{1,0:T(8,128)(2,1)} %get-tuple-element.37) | copy-start | bytes 12582916
  492.9 73.7 %collective-permute-start.3 = (f32[24,128]{1,0:T(8,128)S(1)}, f32[24,128]{1,0:T(8,128)S(1)}, u32[]{:S(2)}, u32[]{:S(2)}) collective-permute-start(f32[24,128]{1,0:T(8,128)S(1)} %pad_maximum_fusion.10), channel_id=1, source_target_pairs={{0,1},{1,0},{2,3},{3,2},{4,5},{5,4},{6,7},{7,6},{8,9},{9,8},{10,11... | collective-permute-start | bytes 36872 | tf_op jit(solution)/shard_map/ppermute | solution.py:268
  498.4 31.3 %copy-start.22 = (bf16[1024,1024]{0,1:T(8,128)(2,1)S(1)}, bf16[1024,1024]{0,1:T(8,128)(2,1)}, u32[]{:S(2)}) copy-start(bf16[1024,1024]{0,1:T(8,128)(2,1)} %copy-done.18) | copy-start | bytes 6291460
  498.4 31.3 %copy-start.36 = (bf16[1024,512]{1,0:T(8,128)(2,1)S(1)}, bf16[1024,512]{1,0:T(8,128)(2,1)}, u32[]{:S(2)}) copy-start(bf16[1024,512]{1,0:T(8,128)(2,1)} %get-tuple-element.36) | copy-start | bytes 3145732
  566.7 2.8 collective-permute-start.4
  569.4 18.4 %collective-permute-start.5 = (f32[24,128]{1,0:T(8,128)S(1)}, f32[24,128]{1,0:T(8,128)S(1)}, u32[]{:S(2)}, u32[]{:S(2)}) collective-permute-start(f32[24,128]{1,0:T(8,128)S(1)} %add.208), channel_id=1, source_target_pairs={{0,4},{2,6},{4,0},{6,2},{8,12},{10,14},{12,8},{14,10},{16,20},{18,... | collective-permute-start | bytes 36872 | tf_op jit(solution)/shard_map/ppermute | solution.py:276
  587.8 3.8 collective-permute-start.6
  591.6 14.0 %collective-permute-start.7 = (f32[24,128]{1,0:T(8,128)S(1)}, f32[24,128]{1,0:T(8,128)S(1)}, u32[]{:S(2)}, u32[]{:S(2)}) collective-permute-start(f32[24,128]{1,0:T(8,128)S(1)} %add.210), channel_id=1, source_target_pairs={{0,16},{2,18},{4,20},{6,22},{8,24},{10,26},{12,28},{14,30},{16,0},... | collective-permute-start | bytes 36872 | tf_op jit(solution)/shard_map/ppermute | solution.py:276
  600.2 7.8 %copy-start.12 = (bf16[64,4736]{1,0:T(8,128)(2,1)S(1)}, bf16[64,4736]{1,0:T(8,128)(2,1)}, u32[]{:S(2)}) copy-start(bf16[64,4736]{1,0:T(8,128)(2,1)} %reduce-scatter.3.cloned.1.call-done) | copy-start | bytes 1818628
  (25 other events, 53.0 us)
Sparse Core Ops, SparseCore 0:
  12.8 80.0 all-gather.2
  95.9 123.2 all-gather.4
  359.1 207.4 reduce-scatter.2
  570.2 70.0 reduce-scatter.4
